TPU v7x, 256 devices: a whole 4x4x8 slice. The times are simulated.
256 devices in a mesh: grp: 4 (over y), cp: 64 (over x, z, core).
Axes of the slice: x: 4, y: 4, z: 8, core: 2. Of those that a mesh axis runs over, the one named last changes fastest.
Arguments:
- queries: bfloat16 [131072, 2048], P(('grp', 'cp')), parts along dimension 0, may hold values from -6 to 6
- keys: bfloat16 [131072, 1024], P(('grp', 'cp')), parts along dimension 0, may hold values from -8 to 8
- values: bfloat16 [131072, 1024], P(('grp', 'cp')), parts along dimension 0, may hold values from -6 to 6
- doc_lengths: int32 [1024], P('grp'), parts along dimension 0, may hold values from 1 to 1024, 32768 in all
Outputs:
- attended: bfloat16 [131072, 2048], P(('grp', 'cp')), parts along dimension 0
There are 4 independent parts, one for each index of `grp`. A program takes and returns all parts, laid end to end along the dimension named above; each array names one. Nothing has to cross between parts.
Inputs may be any that keep to these rules, and one draw needn't show every extreme that they name: doc_lengths sums to 32768, and its largest entry is exactly 1024.
All inputs are finite; a program needn't handle non-finite values.
Results may differ from a plain program's by a relative error of at most 0.0031.
Values may be sent and summed in bfloat16 or wider, within the bound.
A program may use at most 64 MiB of HBM per device.

v0:
```python
import jax
import jax.numpy as jnp
from jax import lax
from jax.sharding import PartitionSpec as P

HQ = 16
HK = 8
DH = 128
REACH = 2


query_scale = 144.0 ** (-0.5)


def shifted(block, axis, distance):
    devices = range(lax.axis_size(axis))
    route = [(i - distance, i) for i in devices if i - distance in devices]
    return lax.ppermute(block, axis, route)


def doc_index(positions, doc_ends):
    return jnp.sum((positions[:, None] >= doc_ends[None, :]).astype(jnp.int32), axis=1)


def on_device(queries, keys, values, doc_lengths):
    tok_rows = queries.shape[0]
    dev_index = lax.axis_index("cp")
    doc_ends = jnp.cumsum(doc_lengths)
    arrived = []
    passed = (keys, values)
    for offset in range(REACH):
        passed = shifted((passed[0], passed[1]), "cp", 1)
        arrived.append(passed)
    ordered = list(reversed(arrived)) + [(keys, values)]
    all_keys = jnp.concatenate([pair[0] for pair in ordered], axis=0)
    all_values = jnp.concatenate([pair[1] for pair in ordered], axis=0)
    first_row = dev_index * tok_rows
    query_pos = first_row + jnp.arange(tok_rows, dtype=jnp.int32)
    key_pos = first_row - REACH * tok_rows + jnp.arange(all_keys.shape[0], dtype=jnp.int32)
    same_doc = doc_index(query_pos, doc_ends)[:, None] == doc_index(key_pos, doc_ends)[None, :]
    visible = same_doc & (key_pos[None, :] <= query_pos[:, None]) & (key_pos[None, :] >= 0)
    groups = HQ // HK
    width = groups * DH

    def one_head(head, result):
        query_part = lax.dynamic_slice_in_dim(queries, head * width, width, 1).reshape(
            tok_rows, groups, DH
        )
        key_part = lax.dynamic_slice_in_dim(all_keys, head * DH, DH, 1)
        value_part = lax.dynamic_slice_in_dim(all_values, head * DH, DH, 1)
        scores = (
            jnp.einsum("tgd,wd->gtw", query_part, key_part, preferred_element_type=jnp.float32)
            * query_scale
        )
        scores = jnp.where(visible[None], scores, -jnp.inf)
        highest = jnp.max(scores, axis=-1, keepdims=True)
        weights = jnp.exp(scores - highest)
        totals = jnp.sum(weights, axis=-1)
        rounded = weights.astype(jnp.bfloat16)
        mixed = jnp.einsum("gtw,wd->tgd", rounded, value_part, preferred_element_type=jnp.float32)
        mixed = mixed / jnp.transpose(totals, (1, 0))[..., None]
        return lax.dynamic_update_slice_in_dim(
            result, mixed.reshape(tok_rows, width).astype(jnp.bfloat16), head * width, 1
        )

    return lax.fori_loop(0, HK, one_head, jnp.zeros_like(queries))


def solution(mesh):
    return jax.shard_map(
        on_device,
        mesh=mesh,
        in_specs=(P(("grp", "cp"), None), P(("grp", "cp"), None), P(("grp", "cp"), None), P("grp")),
        out_specs=P(("grp", "cp"), None),
        check_vma=False,
    )
```

profile of v0, /device:TPU:6, one launch (start us, length us, event | category | flops | bytes accessed | tf_op | source)
XLA Modules:
  0.0 136.8 jit_solution(16757669202044391408)
XLA Ops:
  1.5 1.9 %collective-permute-start = (bf16[512,1024]{0,1:T(8,128)(2,1)S(1)}, bf16[512,1024]{0,1:T(8,128)(2,1)S(1)}, u32[]{:S(2)}, u32[]{:S(2)}) collective-permute-start(bf16[512,1024]{0,1:T(8,128)(2,1)S(1)} %copy.17), channel_id=1, source_target_pairs={{0,1},{1,2},{2,3},{3,4},{4,5},{5,6},{6,7},{7,8},{8,9},{9,10},{10,1... | collective-permute-start | bytes 3145736 | tf_op jit(solution)/shard_map/ppermute | solution.py:18
  3.4 3.9 %collective-permute-start.2 = (bf16[512,1024]{1,0:T(8,128)(2,1)}, bf16[512,1024]{1,0:T(8,128)(2,1)S(1)}, u32[]{:S(2)}, u32[]{:S(2)}) collective-permute-start(bf16[512,1024]{1,0:T(8,128)(2,1)} %param.7), channel_id=1, source_target_pairs={{0,1},{1,2},{2,3},{3,4},{4,5},{5,6},{6,7},{7,8},{8,9},{9,10},{10,1... | collective-permute-start | bytes 3145736 | tf_op jit(solution)/shard_map/ppermute | solution.py:18
  7.4 14.1 %collective-permute-done = bf16[512,1024]{0,1:T(8,128)(2,1)S(1)} collective-permute-done((bf16[512,1024]{0,1:T(8,128)(2,1)S(1)}, bf16[512,1024]{0,1:T(8,128)(2,1)S(1)}, u32[]{:S(2)}, u32[]{:S(2)}) %collective-permute-start) | collective-permute-done | bytes 1048608 | tf_op jit(solution)/shard_map/ppermute | solution.py:18
  21.4 1.9 %collective-permute-start.1 = (bf16[512,1024]{0,1:T(8,128)(2,1)S(1)}, bf16[512,1024]{0,1:T(8,128)(2,1)}, u32[]{:S(2)}, u32[]{:S(2)}) collective-permute-start(bf16[512,1024]{0,1:T(8,128)(2,1)S(1)} %collective-permute-done), channel_id=1, source_target_pairs={{0,1},{1,2},{2,3},{3,4},{4,5},{5,6},{6,7},{7,8},{8,9},{9,10},{10,1... | collective-permute-start | bytes 3145736 | tf_op jit(solution)/shard_map/ppermute | solution.py:18
  23.4 9.3 %collective-permute-done.2 = bf16[512,1024]{1,0:T(8,128)(2,1)S(1)} collective-permute-done((bf16[512,1024]{1,0:T(8,128)(2,1)}, bf16[512,1024]{1,0:T(8,128)(2,1)S(1)}, u32[]{:S(2)}, u32[]{:S(2)}) %collective-permute-start.2) | collective-permute-done | bytes 1048608 | tf_op jit(solution)/shard_map/ppermute | solution.py:18
  32.7 1.9 %collective-permute-start.3 = (bf16[512,1024]{1,0:T(8,128)(2,1)S(1)}, bf16[512,1024]{1,0:T(8,128)(2,1)}, u32[]{:S(2)}, u32[]{:S(2)}) collective-permute-start(bf16[512,1024]{1,0:T(8,128)(2,1)S(1)} %collective-permute-done.2), channel_id=1, source_target_pairs={{0,1},{1,2},{2,3},{3,4},{4,5},{5,6},{6,7},{7,8},{8,9},{9,10},{10,1... | collective-permute-start | bytes 3145736 | tf_op jit(solution)/shard_map/ppermute | solution.py:18
  36.6 7.4 %collective-permute-done.1 = bf16[512,1024]{0,1:T(8,128)(2,1)} collective-permute-done((bf16[512,1024]{0,1:T(8,128)(2,1)S(1)}, bf16[512,1024]{0,1:T(8,128)(2,1)}, u32[]{:S(2)}, u32[]{:S(2)}) %collective-permute-start.1) | collective-permute-done | bytes 1048608 | tf_op jit(solution)/shard_map/ppermute | solution.py:18
  44.0 2.8 %pad_maximum_fusion = bf16[1536,1024]{0,1:T(8,128)(2,1)} fusion(bf16[512,1024]{0,1:T(8,128)(2,1)S(1)} %copy.17, bf16[512,1024]{0,1:T(8,128)(2,1)S(1)} %collective-permute-done, bf16[512,1024]{0,1:T(8,128)(2,1)} %collective-permute-done.1), kind=kLoop, calls=%fused_computation.23 | loop fusion | flops 9437184 | bytes 6291456 | tf_op jit(solution)/shard_map/concatenate | solution.py:36
  46.8 8.4 %collective-permute-done.3 = bf16[512,1024]{1,0:T(8,128)(2,1)} collective-permute-done((bf16[512,1024]{1,0:T(8,128)(2,1)S(1)}, bf16[512,1024]{1,0:T(8,128)(2,1)}, u32[]{:S(2)}, u32[]{:S(2)}) %collective-permute-start.3) | collective-permute-done | bytes 1048608 | tf_op jit(solution)/shard_map/ppermute | solution.py:18
  55.3 2.9 %pad_maximum_fusion.1 = bf16[1536,1024]{1,0:T(8,128)(2,1)} fusion(bf16[512,1024]{1,0:T(8,128)(2,1)S(1)} %copy-done.1, bf16[512,1024]{1,0:T(8,128)(2,1)S(1)} %collective-permute-done.2, bf16[512,1024]{1,0:T(8,128)(2,1)} %collective-permute-done.3), kind=kLoop, calls=%fused_computation.24 | loop fusion | flops 9437184 | bytes 6291456 | tf_op jit(solution)/shard_map/concatenate | solution.py:35
  58.4 77.0 %while.14 = (s32[]{:T(128)}, bf16[512,2048]{1,0:T(8,128)(2,1)S(1)}, bf16[1536,1024]{0,1:T(8,128)(2,1)}, bf16[1536,1024]{1,0:T(8,128)(2,1)}, bf16[512,2048]{1,0:T...) while((s32[]{:T(128)}, bf16[512,2048]{1,0:T(8,128)(2,1)S(1)}, ...), condition=%wide.region_7.8_spmd.clone, body=%wide.region_4.0_spmd.clone.sunk | while | flops 826013696 | bytes 25466632 | solution.py:66
  59.6 1.5 %and_and_fusion.2 = pred[512,1536]{0,1:T(8,128)(4,1)S(1)} fusion(s32[512]{0:T(512)S(1)} %get-tuple-element.288, s32[512]{0:T(512)S(1)} %get-tuple-element.287, s32[1536]{0:T(1024)S(1)} %get-tuple-element.289, s32[1536]{0:T(1024)S(1)} %get-tuple-element.286, pred[1536]{0:T(1024)(128)(4,1)S(1)} %get-tuple-element.290), kind=kLoop, calls=%fused_computation.7.clone.1 | loop fusion | flops 3145728 | bytes 804352 | tf_op jit(solution)/shard_map/and | solution.py:41
  61.1 2.3 %fusion.36 = (f32[2,512]{1,0:T(2,128)S(1)}, f32[1536,512,2]{1,0,2:T(8,128)S(1)}) fusion(pred[512,1536]{0,1:T(8,128)(4,1)S(1)} %and_and_fusion.2, bf16[512,2,128]{0,2,1:T(8,128)(2,1)S(1)} %bitcast.57, bf16[1536,1024]{1,0:T(8,128)(2,1)} %get-tuple-element.284, s32[]{:T(128)S(6)} %select_n.50), kind=kOutput, calls=%fused_computation.5.clone.1 | convolution fusion | flops 407370752 | bytes 7737348 | tf_op jit(solution)/shard_map/while/body/eval_jaxpr/tgd,wd->gtw/dot_general | solution.py:52
  64.9 3.0 %fusion.38 = bf16[512,2,128]{0,2,1:T(8,128)(2,1)S(1)} fusion(f32[1536,512,2]{1,0,2:T(8,128)S(1)} %get-tuple-element.247, f32[2,512]{1,0:T(2,128)S(1)} %get-tuple-element.248, pred[512,1536]{0,1:T(8,128)(4,1)S(1)} %and_and_fusion.2, bf16[1536,1024]{0,1:T(8,128)(2,1)} %get-tuple-element.283, s32[]{:T(128)S(6)} %select_n.50, f32[512,2]{0,1:T(2,128)S(1)} %bitcast.58), kind=kOutput, calls=%fused_computation.11.clone.1 | convolution fusion | flops 409206784 | bytes 7741444 | tf_op jit(solution)/shard_map/while/body/eval_jaxpr/gtw,wd->tgd/dot_general | solution.py:60
  69.2 1.5 %and_and_fusion.2 = pred[512,1536]{0,1:T(8,128)(4,1)S(1)} fusion(s32[512]{0:T(512)S(1)} %get-tuple-element.288, s32[512]{0:T(512)S(1)} %get-tuple-element.287, s32[1536]{0:T(1024)S(1)} %get-tuple-element.289, s32[1536]{0:T(1024)S(1)} %get-tuple-element.286, pred[1536]{0:T(1024)(128)(4,1)S(1)} %get-tuple-element.290), kind=kLoop, calls=%fused_computation.7.clone.1 | loop fusion | flops 3145728 | bytes 804352 | tf_op jit(solution)/shard_map/and | solution.py:41
  70.7 2.3 %fusion.36 = (f32[2,512]{1,0:T(2,128)S(1)}, f32[1536,512,2]{1,0,2:T(8,128)S(1)}) fusion(pred[512,1536]{0,1:T(8,128)(4,1)S(1)} %and_and_fusion.2, bf16[512,2,128]{0,2,1:T(8,128)(2,1)S(1)} %bitcast.57, bf16[1536,1024]{1,0:T(8,128)(2,1)} %get-tuple-element.284, s32[]{:T(128)S(6)} %select_n.50), kind=kOutput, calls=%fused_computation.5.clone.1 | convolution fusion | flops 407370752 | bytes 7737348 | tf_op jit(solution)/shard_map/while/body/eval_jaxpr/tgd,wd->gtw/dot_general | solution.py:52
  74.5 3.0 %fusion.38 = bf16[512,2,128]{0,2,1:T(8,128)(2,1)S(1)} fusion(f32[1536,512,2]{1,0,2:T(8,128)S(1)} %get-tuple-element.247, f32[2,512]{1,0:T(2,128)S(1)} %get-tuple-element.248, pred[512,1536]{0,1:T(8,128)(4,1)S(1)} %and_and_fusion.2, bf16[1536,1024]{0,1:T(8,128)(2,1)} %get-tuple-element.283, s32[]{:T(128)S(6)} %select_n.50, f32[512,2]{0,1:T(2,128)S(1)} %bitcast.58), kind=kOutput, calls=%fused_computation.11.clone.1 | convolution fusion | flops 409206784 | bytes 7741444 | tf_op jit(solution)/shard_map/while/body/eval_jaxpr/gtw,wd->tgd/dot_general | solution.py:60
  78.8 1.5 %and_and_fusion.2 = pred[512,1536]{0,1:T(8,128)(4,1)S(1)} fusion(s32[512]{0:T(512)S(1)} %get-tuple-element.288, s32[512]{0:T(512)S(1)} %get-tuple-element.287, s32[1536]{0:T(1024)S(1)} %get-tuple-element.289, s32[1536]{0:T(1024)S(1)} %get-tuple-element.286, pred[1536]{0:T(1024)(128)(4,1)S(1)} %get-tuple-element.290), kind=kLoop, calls=%fused_computation.7.clone.1 | loop fusion | flops 3145728 | bytes 804352 | tf_op jit(solution)/shard_map/and | solution.py:41
  80.4 2.3 %fusion.36 = (f32[2,512]{1,0:T(2,128)S(1)}, f32[1536,512,2]{1,0,2:T(8,128)S(1)}) fusion(pred[512,1536]{0,1:T(8,128)(4,1)S(1)} %and_and_fusion.2, bf16[512,2,128]{0,2,1:T(8,128)(2,1)S(1)} %bitcast.57, bf16[1536,1024]{1,0:T(8,128)(2,1)} %get-tuple-element.284, s32[]{:T(128)S(6)} %select_n.50), kind=kOutput, calls=%fused_computation.5.clone.1 | convolution fusion | flops 407370752 | bytes 7737348 | tf_op jit(solution)/shard_map/while/body/eval_jaxpr/tgd,wd->gtw/dot_general | solution.py:52
  84.1 3.0 %fusion.38 = bf16[512,2,128]{0,2,1:T(8,128)(2,1)S(1)} fusion(f32[1536,512,2]{1,0,2:T(8,128)S(1)} %get-tuple-element.247, f32[2,512]{1,0:T(2,128)S(1)} %get-tuple-element.248, pred[512,1536]{0,1:T(8,128)(4,1)S(1)} %and_and_fusion.2, bf16[1536,1024]{0,1:T(8,128)(2,1)} %get-tuple-element.283, s32[]{:T(128)S(6)} %select_n.50, f32[512,2]{0,1:T(2,128)S(1)} %bitcast.58), kind=kOutput, calls=%fused_computation.11.clone.1 | convolution fusion | flops 409206784 | bytes 7741444 | tf_op jit(solution)/shard_map/while/body/eval_jaxpr/gtw,wd->tgd/dot_general | solution.py:60
  88.4 1.5 %and_and_fusion.2 = pred[512,1536]{0,1:T(8,128)(4,1)S(1)} fusion(s32[512]{0:T(512)S(1)} %get-tuple-element.288, s32[512]{0:T(512)S(1)} %get-tuple-element.287, s32[1536]{0:T(1024)S(1)} %get-tuple-element.289, s32[1536]{0:T(1024)S(1)} %get-tuple-element.286, pred[1536]{0:T(1024)(128)(4,1)S(1)} %get-tuple-element.290), kind=kLoop, calls=%fused_computation.7.clone.1 | loop fusion | flops 3145728 | bytes 804352 | tf_op jit(solution)/shard_map/and | solution.py:41
  90.0 2.3 %fusion.36 = (f32[2,512]{1,0:T(2,128)S(1)}, f32[1536,512,2]{1,0,2:T(8,128)S(1)}) fusion(pred[512,1536]{0,1:T(8,128)(4,1)S(1)} %and_and_fusion.2, bf16[512,2,128]{0,2,1:T(8,128)(2,1)S(1)} %bitcast.57, bf16[1536,1024]{1,0:T(8,128)(2,1)} %get-tuple-element.284, s32[]{:T(128)S(6)} %select_n.50), kind=kOutput, calls=%fused_computation.5.clone.1 | convolution fusion | flops 407370752 | bytes 7737348 | tf_op jit(solution)/shard_map/while/body/eval_jaxpr/tgd,wd->gtw/dot_general | solution.py:52
  93.8 3.0 %fusion.38 = bf16[512,2,128]{0,2,1:T(8,128)(2,1)S(1)} fusion(f32[1536,512,2]{1,0,2:T(8,128)S(1)} %get-tuple-element.247, f32[2,512]{1,0:T(2,128)S(1)} %get-tuple-element.248, pred[512,1536]{0,1:T(8,128)(4,1)S(1)} %and_and_fusion.2, bf16[1536,1024]{0,1:T(8,128)(2,1)} %get-tuple-element.283, s32[]{:T(128)S(6)} %select_n.50, f32[512,2]{0,1:T(2,128)S(1)} %bitcast.58), kind=kOutput, calls=%fused_computation.11.clone.1 | convolution fusion | flops 409206784 | bytes 7741444 | tf_op jit(solution)/shard_map/while/body/eval_jaxpr/gtw,wd->tgd/dot_general | solution.py:60
  98.1 1.5 %and_and_fusion.2 = pred[512,1536]{0,1:T(8,128)(4,1)S(1)} fusion(s32[512]{0:T(512)S(1)} %get-tuple-element.288, s32[512]{0:T(512)S(1)} %get-tuple-element.287, s32[1536]{0:T(1024)S(1)} %get-tuple-element.289, s32[1536]{0:T(1024)S(1)} %get-tuple-element.286, pred[1536]{0:T(1024)(128)(4,1)S(1)} %get-tuple-element.290), kind=kLoop, calls=%fused_computation.7.clone.1 | loop fusion | flops 3145728 | bytes 804352 | tf_op jit(solution)/shard_map/and | solution.py:41
  99.6 2.3 %fusion.36 = (f32[2,512]{1,0:T(2,128)S(1)}, f32[1536,512,2]{1,0,2:T(8,128)S(1)}) fusion(pred[512,1536]{0,1:T(8,128)(4,1)S(1)} %and_and_fusion.2, bf16[512,2,128]{0,2,1:T(8,128)(2,1)S(1)} %bitcast.57, bf16[1536,1024]{1,0:T(8,128)(2,1)} %get-tuple-element.284, s32[]{:T(128)S(6)} %select_n.50), kind=kOutput, calls=%fused_computation.5.clone.1 | convolution fusion | flops 407370752 | bytes 7737348 | tf_op jit(solution)/shard_map/while/body/eval_jaxpr/tgd,wd->gtw/dot_general | solution.py:52
  103.4 3.0 %fusion.38 = bf16[512,2,128]{0,2,1:T(8,128)(2,1)S(1)} fusion(f32[1536,512,2]{1,0,2:T(8,128)S(1)} %get-tuple-element.247, f32[2,512]{1,0:T(2,128)S(1)} %get-tuple-element.248, pred[512,1536]{0,1:T(8,128)(4,1)S(1)} %and_and_fusion.2, bf16[1536,1024]{0,1:T(8,128)(2,1)} %get-tuple-element.283, s32[]{:T(128)S(6)} %select_n.50, f32[512,2]{0,1:T(2,128)S(1)} %bitcast.58), kind=kOutput, calls=%fused_computation.11.clone.1 | convolution fusion | flops 409206784 | bytes 7741444 | tf_op jit(solution)/shard_map/while/body/eval_jaxpr/gtw,wd->tgd/dot_general | solution.py:60
  109.2 2.3 %fusion.36 = (f32[2,512]{1,0:T(2,128)S(1)}, f32[1536,512,2]{1,0,2:T(8,128)S(1)}) fusion(pred[512,1536]{0,1:T(8,128)(4,1)S(1)} %and_and_fusion.2, bf16[512,2,128]{0,2,1:T(8,128)(2,1)S(1)} %bitcast.57, bf16[1536,1024]{1,0:T(8,128)(2,1)} %get-tuple-element.284, s32[]{:T(128)S(6)} %select_n.50), kind=kOutput, calls=%fused_computation.5.clone.1 | convolution fusion | flops 407370752 | bytes 7737348 | tf_op jit(solution)/shard_map/while/body/eval_jaxpr/tgd,wd->gtw/dot_general | solution.py:52
  113.0 3.0 %fusion.38 = bf16[512,2,128]{0,2,1:T(8,128)(2,1)S(1)} fusion(f32[1536,512,2]{1,0,2:T(8,128)S(1)} %get-tuple-element.247, f32[2,512]{1,0:T(2,128)S(1)} %get-tuple-element.248, pred[512,1536]{0,1:T(8,128)(4,1)S(1)} %and_and_fusion.2, bf16[1536,1024]{0,1:T(8,128)(2,1)} %get-tuple-element.283, s32[]{:T(128)S(6)} %select_n.50, f32[512,2]{0,1:T(2,128)S(1)} %bitcast.58), kind=kOutput, calls=%fused_computation.11.clone.1 | convolution fusion | flops 409206784 | bytes 7741444 | tf_op jit(solution)/shard_map/while/body/eval_jaxpr/gtw,wd->tgd/dot_general | solution.py:60
  118.9 2.3 %fusion.36 = (f32[2,512]{1,0:T(2,128)S(1)}, f32[1536,512,2]{1,0,2:T(8,128)S(1)}) fusion(pred[512,1536]{0,1:T(8,128)(4,1)S(1)} %and_and_fusion.2, bf16[512,2,128]{0,2,1:T(8,128)(2,1)S(1)} %bitcast.57, bf16[1536,1024]{1,0:T(8,128)(2,1)} %get-tuple-element.284, s32[]{:T(128)S(6)} %select_n.50), kind=kOutput, calls=%fused_computation.5.clone.1 | convolution fusion | flops 407370752 | bytes 7737348 | tf_op jit(solution)/shard_map/while/body/eval_jaxpr/tgd,wd->gtw/dot_general | solution.py:52
  122.6 3.0 %fusion.38 = bf16[512,2,128]{0,2,1:T(8,128)(2,1)S(1)} fusion(f32[1536,512,2]{1,0,2:T(8,128)S(1)} %get-tuple-element.247, f32[2,512]{1,0:T(2,128)S(1)} %get-tuple-element.248, pred[512,1536]{0,1:T(8,128)(4,1)S(1)} %and_and_fusion.2, bf16[1536,1024]{0,1:T(8,128)(2,1)} %get-tuple-element.283, s32[]{:T(128)S(6)} %select_n.50, f32[512,2]{0,1:T(2,128)S(1)} %bitcast.58), kind=kOutput, calls=%fused_computation.11.clone.1 | convolution fusion | flops 409206784 | bytes 7741444 | tf_op jit(solution)/shard_map/while/body/eval_jaxpr/gtw,wd->tgd/dot_general | solution.py:60
  128.5 2.3 %fusion.36 = (f32[2,512]{1,0:T(2,128)S(1)}, f32[1536,512,2]{1,0,2:T(8,128)S(1)}) fusion(pred[512,1536]{0,1:T(8,128)(4,1)S(1)} %and_and_fusion.2, bf16[512,2,128]{0,2,1:T(8,128)(2,1)S(1)} %bitcast.57, bf16[1536,1024]{1,0:T(8,128)(2,1)} %get-tuple-element.284, s32[]{:T(128)S(6)} %select_n.50), kind=kOutput, calls=%fused_computation.5.clone.1 | convolution fusion | flops 407370752 | bytes 7737348 | tf_op jit(solution)/shard_map/while/body/eval_jaxpr/tgd,wd->gtw/dot_general | solution.py:52
  132.3 3.0 %fusion.38 = bf16[512,2,128]{0,2,1:T(8,128)(2,1)S(1)} fusion(f32[1536,512,2]{1,0,2:T(8,128)S(1)} %get-tuple-element.247, f32[2,512]{1,0:T(2,128)S(1)} %get-tuple-element.248, pred[512,1536]{0,1:T(8,128)(4,1)S(1)} %and_and_fusion.2, bf16[1536,1024]{0,1:T(8,128)(2,1)} %get-tuple-element.283, s32[]{:T(128)S(6)} %select_n.50, f32[512,2]{0,1:T(2,128)S(1)} %bitcast.58), kind=kOutput, calls=%fused_computation.11.clone.1 | convolution fusion | flops 409206784 | bytes 7741444 | tf_op jit(solution)/shard_map/while/body/eval_jaxpr/gtw,wd->tgd/dot_general | solution.py:60
  (59 shorter events, 31.4 us)
Async XLA Ops:
  1.5 19.9 %collective-permute-start = (bf16[512,1024]{0,1:T(8,128)(2,1)S(1)}, bf16[512,1024]{0,1:T(8,128)(2,1)S(1)}, u32[]{:S(2)}, u32[]{:S(2)}) collective-permute-start(bf16[512,1024]{0,1:T(8,128)(2,1)S(1)} %copy.17), channel_id=1, source_target_pairs={{0,1},{1,2},{2,3},{3,4},{4,5},{5,6},{6,7},{7,8},{8,9},{9,10},{10,1... | collective-permute-start | bytes 3145736 | tf_op jit(solution)/shard_map/ppermute | solution.py:18
  3.4 29.3 %collective-permute-start.2 = (bf16[512,1024]{1,0:T(8,128)(2,1)}, bf16[512,1024]{1,0:T(8,128)(2,1)S(1)}, u32[]{:S(2)}, u32[]{:S(2)}) collective-permute-start(bf16[512,1024]{1,0:T(8,128)(2,1)} %param.7), channel_id=1, source_target_pairs={{0,1},{1,2},{2,3},{3,4},{4,5},{5,6},{6,7},{7,8},{8,9},{9,10},{10,1... | collective-permute-start | bytes 3145736 | tf_op jit(solution)/shard_map/ppermute | solution.py:18
  21.4 22.6 %collective-permute-start.1 = (bf16[512,1024]{0,1:T(8,128)(2,1)S(1)}, bf16[512,1024]{0,1:T(8,128)(2,1)}, u32[]{:S(2)}, u32[]{:S(2)}) collective-permute-start(bf16[512,1024]{0,1:T(8,128)(2,1)S(1)} %collective-permute-done), channel_id=1, source_target_pairs={{0,1},{1,2},{2,3},{3,4},{4,5},{5,6},{6,7},{7,8},{8,9},{9,10},{10,1... | collective-permute-start | bytes 3145736 | tf_op jit(solution)/shard_map/ppermute | solution.py:18
  32.7 22.6 %collective-permute-start.3 = (bf16[512,1024]{1,0:T(8,128)(2,1)S(1)}, bf16[512,1024]{1,0:T(8,128)(2,1)}, u32[]{:S(2)}, u32[]{:S(2)}) collective-permute-start(bf16[512,1024]{1,0:T(8,128)(2,1)S(1)} %collective-permute-done.2), channel_id=1, source_target_pairs={{0,1},{1,2},{2,3},{3,4},{4,5},{5,6},{6,7},{7,8},{8,9},{9,10},{10,1... | collective-permute-start | bytes 3145736 | tf_op jit(solution)/shard_map/ppermute | solution.py:18
  36.6 18.6 %copy-start.1 = (bf16[512,1024]{1,0:T(8,128)(2,1)S(1)}, bf16[512,1024]{1,0:T(8,128)(2,1)}, u32[]{:S(2)}) copy-start(bf16[512,1024]{1,0:T(8,128)(2,1)} %param.7) | copy-start | bytes 3145732
  135.4 1.3 copy-start
where the time goes:
time: 138 us; the launch traced here: 137 us
  matrix products  42.5 us (31%)
  waiting for transfers between devices  39.2 us (28%)
  other arithmetic  31.3 us (23%)
  local copies, waits for them, and re-layouts  13.4 us (10%)
  starting transfers between devices  9.67 us (7%)
    ppermute x4, waiting for transfers between devices, shifted(): return lax.ppermute(block, axis, route)  39.2 us
    dot_general x8, matrix products, one_head(): jnp.einsum('gtw,wd->tgd', rounded, value_part, preferred_element_type=jnp...  23.9 us
    dot_general x8, matrix products, one_head(): jnp.einsum('tgd,wd->gtw', query_part, key_part, preferred_element_type=jn...  18.6 us
    and x8, other arithmetic, on_device(): same_doc & (key_pos[None, :] <= query_pos[:, None])  12.2 us
    reduce_sum x8, other arithmetic, one_head(): totals = jnp.sum(weights, axis=-1)  11.5 us
    ppermute x4, starting transfers between devices, shifted(): return lax.ppermute(block, axis, route)  9.67 us
    dynamic_slice x16, local copies, waits for them, and re-layouts, one_head(): lax.dynamic_slice_in_dim(queries, head * width, width, 1)  8.91 us
    concatenate x1, other arithmetic, on_device(): all_keys = jnp.concatenate([pair[0] for pair in ordered], axis=0)  2.91 us
  transfers between devices with their start and end apart: 4, of which 4 were waited for; matrix products, arithmetic and copies ran while one was open for 4% of the time, Pallas kernels for 0%

commit v1 on v0

v1 whole, which is shorter than its diff:
```python
import functools
import math

import jax
import jax.numpy as jnp
from jax import lax
from jax.experimental import pallas as pl
from jax.experimental.pallas import tpu as pltpu
from jax.sharding import PartitionSpec as P

DH = 128
T = 512
B = 128
LAG = 2
BIG = 32768.0
NEG = -1e30
SCALE = 144.0 ** (-0.5) * math.log2(math.e)
MESH = pl.DeviceIdType.MESH
F32, BF16, I32 = jnp.float32, jnp.bfloat16, jnp.int32


def stacked(pair):
    return jnp.concatenate([pair[:, :DH], pair[:, DH:]], axis=0)


def unstacked(x):
    return jnp.concatenate([x[:B], x[B:]], axis=1)


def kernel(
    q_hbm, k_hbm, v_hbm, len_ref, o_hbm,
    kv, qv, qr, msg, outv, stat_s, stat_r, augk, augq, augr, flags,
    loc_sem, q_send, q_recv, own_send, own_recv, msg_send, msg_recv,
    st_send, st_recv, fwd_send, fwd_recv, out_sem,
):
    hk = kv.shape[0]
    n = lax.axis_size("cp")
    me = lax.axis_index("cp")
    core = lax.rem(me, 2)
    chip = lax.div(me, 2)
    partner = me + 1 - 2 * core
    after = lax.rem(me + 2, n)
    before = lax.rem(me + n - 2, n)
    own0 = pl.multiple_of(T + T * core, T)
    barrier = pltpu.get_barrier_semaphore()

    def local(h):
        lo = pl.ds(pl.multiple_of(h * DH, DH), DH)
        two = pl.ds(pl.multiple_of(h * 2 * DH, DH), 2 * DH)
        mine = pl.ds(own0, T)
        return (
            pltpu.make_async_copy(k_hbm.at[:, lo], kv.at[h, mine, pl.ds(0, DH)], loc_sem.at[0, h]),
            pltpu.make_async_copy(v_hbm.at[:, lo], kv.at[h, mine, pl.ds(DH, DH)], loc_sem.at[1, h]),
            pltpu.make_async_copy(q_hbm.at[:, two], qv.at[h], loc_sem.at[2, h]),
        )

    def remote(src, dst, send, recv, to):
        return pltpu.make_async_remote_copy(src, dst, send, recv, device_id={"cp": to}, device_id_type=MESH)

    def send_q(h):
        two = pl.ds(pl.multiple_of(h * 2 * DH, DH), 2 * DH)
        return remote(q_hbm.at[:, two], qr.at[h], q_send.at[h], q_recv.at[h], before)

    def send_own(h):
        mine = kv.at[h, pl.ds(own0, T)]
        return remote(mine, mine, own_send.at[h], own_recv.at[h], partner)

    def send_msg(h):
        return remote(msg.at[h], kv.at[h, pl.ds(0, T)], msg_send.at[h], msg_recv.at[h], after)

    def send_stat(h):
        return remote(stat_s.at[h], stat_r.at[h], st_send.at[h], st_recv.at[h], after)

    def forward(h):
        part = kv.at[h, pl.ds(0, T)]
        return remote(part, part, fwd_send.at[h], fwd_recv.at[h], partner)

    def put(h):
        two = pl.ds(pl.multiple_of(h * 2 * DH, DH), 2 * DH)
        return pltpu.make_async_copy(outv.at[h], o_hbm.at[:, two], out_sem.at[h])

    def every(body):
        def step(h, carry):
            body(h)
            return carry

        lax.fori_loop(0, hk, step, 0)

    @pl.when(core == 0)
    def _():
        for other in (before, after, partner):
            pl.semaphore_signal(barrier, inc=1, device_id={"cp": other}, device_id_type=MESH)
        pl.semaphore_wait(barrier, 3)
        every(lambda h: send_q(h).start())

    @pl.when(core == 1)
    def _():
        pl.semaphore_signal(barrier, inc=1, device_id={"cp": partner}, device_id_type=MESH)
        pl.semaphore_wait(barrier, 1)

    def start_local(h):
        for copy in local(h):
            copy.start()

    every(start_local)

    lens = jnp.broadcast_to(len_ref[...], (8, len_ref.shape[1]))
    docs = lens.shape[1]
    upto = lax.broadcasted_iota(I32, (docs, docs), 0) <= lax.broadcasted_iota(I32, (docs, docs), 1)
    upto = jnp.where(upto, 1.0, 0.0).astype(BF16)
    high = lax.shift_right_logical(lens, 5).astype(F32).astype(BF16)
    low = (lens & 31).astype(F32).astype(BF16)
    ends = 32.0 * jnp.dot(high, upto, preferred_element_type=F32) + jnp.dot(low, upto, preferred_element_type=F32)
    ends = ends[0:1].astype(I32)
    ones = jnp.ones((docs, DH), BF16)

    def doc_of(pos):
        past = jnp.where(pos >= ends, 1.0, 0.0).astype(BF16)
        return jnp.dot(past, ones, preferred_element_type=F32)

    def doc_rows(base, rows):
        return doc_of(lax.broadcasted_iota(I32, (rows, docs), 0) + base)

    def doc_at(p):
        return doc_of(jnp.zeros((8, docs), I32) + p)

    def bits(doc):
        lane = lax.broadcasted_iota(I32, doc.shape, 1)
        return (lax.shift_right_logical(doc.astype(I32), lane & 7) & 1).astype(F32), lane

    def key_side(doc, hidden):
        b, lane = bits(doc)
        out = jnp.where(lane < 8, b - 1.0, jnp.where(lane < 16, -b, jnp.where(lane == 16, -hidden, 0.0)))
        return (out * BIG).astype(BF16)

    def query_side(doc):
        b, lane = bits(doc)
        return jnp.where(lane < 8, b, jnp.where(lane < 16, 1.0 - b, jnp.where(lane == 16, 1.0, 0.0))).astype(BF16)

    first = chip * (2 * T)
    inner = jnp.where(chip > 0, 1.0, 0.0)
    far_left = jnp.where(doc_at(first - T - 1) == doc_at(first), 1.0, 0.0) * inner
    far_right = jnp.where(doc_at(first + T - 1) == doc_at(first + 2 * T), 1.0, 0.0)
    flags[0] = far_left
    flags[1] = far_right
    hidden = jnp.maximum(far_left, 1.0 - inner)[0:1]
    for part in range(3):
        doc = doc_rows(first + (part - 1) * T, T)
        augk[part * T : (part + 1) * T] = key_side(doc, hidden if part == 0 else 0.0)
    augq[...] = query_side(doc_rows(me * T, T))
    augr[...] = query_side(doc_rows(first + 2 * T, T))

    ones_v = jnp.ones((3 * T, DH), BF16)
    row = lax.broadcasted_iota(I32, (2 * B, B), 0)
    causal = lax.broadcasted_iota(I32, (2 * B, B), 1) <= (row & (B - 1))

    def scores(h, pair, aug, lo, hi):
        q = jnp.concatenate([stacked(pair), jnp.concatenate([aug, aug], axis=0)], axis=1)
        k = jnp.concatenate([kv[h, lo:hi, 0:DH], augk[lo:hi]], axis=1)
        return lax.dot_general(q, k, (((1,), (1,)), ((), ())), preferred_element_type=F32)

    def mixed(h, s, top, lo, hi):
        p = jnp.exp2(s * SCALE - top).astype(BF16)
        v = jnp.concatenate([kv[h, lo:hi, DH : 2 * DH], ones_v[: hi - lo]], axis=1)
        o = jnp.dot(p, v, preferred_element_type=F32)
        return o[:, :DH], o[:, DH:]

    def masked(s):
        return jnp.concatenate([s[:, :-B], jnp.where(causal, s[:, -B:], NEG)], axis=1)

    def border_block(h, r):
        rows = slice(r * B, (r + 1) * B)
        lo, hi = T + r * B, 3 * T
        s = scores(h, qr[h, rows], augr[rows], lo, hi)
        top = jnp.max(s, axis=1, keepdims=True) * SCALE
        acc, total = mixed(h, s, top, lo, hi)
        partial = unstacked(acc / total)
        own = kv[h, 2 * T + r * B : 2 * T + (r + 1) * B].astype(F32)
        msg[h, rows] = jnp.where(flags[1][0:1, 0:1] > 0.5, partial, own).astype(BF16)
        level = top + jnp.log2(total)
        even = (lax.broadcasted_iota(I32, (B, DH), 1) & 1) == 0
        stat_s[h, :, rows] = jnp.transpose(jnp.where(even, level[:B], level[B:]))[0:8]

    def head_block(h, r):
        rows = slice(r * B, (r + 1) * B)
        hi = T + (r + 1) * B
        s = masked(scores(h, qv[h, rows], augq[rows], 0, hi))
        level = jnp.concatenate(
            [jnp.transpose(jnp.broadcast_to(stat_r[h, i : i + 1, rows], (DH, B))) for i in range(2)], axis=0
        )
        level = jnp.where(flags[0][0:1] > 0.5, level, NEG)
        top = jnp.maximum(jnp.max(s, axis=1, keepdims=True) * SCALE, level[:, 0:1])
        acc, total = mixed(h, s, top, 0, hi)
        weight = jnp.exp2(level - top)
        other = stacked(kv[h, rows]).astype(F32)
        outv[h, rows] = unstacked((acc + weight * other) / (total + weight)).astype(BF16)

    def tail_block(h, r):
        rows = slice(r * B, (r + 1) * B)
        lo, hi = r * B, 2 * T + (r + 1) * B
        s = masked(scores(h, qv[h, rows], augq[rows], lo, hi))
        top = jnp.max(s, axis=1, keepdims=True) * SCALE
        acc, total = mixed(h, s, top, lo, hi)
        outv[h, rows] = unstacked(acc / total).astype(BF16)

    def share(h):
        for copy in local(h):
            copy.wait()
        send_own(h).start()

    every(share)

    @pl.when(core == 0)
    def _():
        def step(it, carry):
            @pl.when(it < hk)
            def _():
                send_q(it).wait_recv()
                send_own(it).wait_recv()
                for r in range(T // B):
                    border_block(it, r)
                send_msg(it).start()
                send_stat(it).start()

            @pl.when(it >= LAG)
            def _():
                h = it - LAG
                send_msg(h).wait_recv()
                send_stat(h).wait_recv()
                forward(h).start()
                for r in range(T // B):
                    head_block(h, r)
                put(h).start()

            return carry

        lax.fori_loop(0, hk + LAG, step, 0)

        def finish(h):
            send_q(h).wait_send()
            send_own(h).wait_send()
            send_msg(h).wait_send()
            send_stat(h).wait_send()
            forward(h).wait_send()
            put(h).wait()

        every(finish)

    @pl.when(core == 1)
    def _():
        def step(h):
            send_own(h).wait_recv()
            forward(h).wait_recv()
            for r in range(T // B):
                tail_block(h, r)
            put(h).start()

        every(step)

        def finish(h):
            send_own(h).wait_send()
            put(h).wait()

        every(finish)


def on_device(queries, keys, values, doc_lengths):
    hk = keys.shape[1] // DH
    docs = doc_lengths.shape[0]
    sem = pltpu.SemaphoreType.DMA
    any_spec = pl.BlockSpec(memory_space=pl.ANY)
    return pl.pallas_call(
        kernel,
        out_shape=jax.ShapeDtypeStruct(queries.shape, BF16),
        in_specs=[any_spec, any_spec, any_spec, pl.BlockSpec(memory_space=pltpu.VMEM)],
        out_specs=any_spec,
        scratch_shapes=[
            pltpu.VMEM((hk, 3 * T, 2 * DH), BF16),
            pltpu.VMEM((hk, T, 2 * DH), BF16),
            pltpu.VMEM((hk, T, 2 * DH), BF16),
            pltpu.VMEM((hk, T, 2 * DH), BF16),
            pltpu.VMEM((hk, T, 2 * DH), BF16),
            pltpu.VMEM((hk, 8, T), F32),
            pltpu.VMEM((hk, 8, T), F32),
            pltpu.VMEM((3 * T, DH), BF16),
            pltpu.VMEM((T, DH), BF16),
            pltpu.VMEM((T, DH), BF16),
            pltpu.VMEM((2, 8, DH), F32),
            sem((3, hk)),
        ]
        + [sem((hk,))] * 11,
        compiler_params=pltpu.CompilerParams(
            collective_id=0, has_side_effects=True, vmem_limit_bytes=60 * 1024 * 1024
        ),
    )(queries, keys, values, doc_lengths.reshape(1, docs))


def solution(mesh):
    return jax.shard_map(
        on_device,
        mesh=mesh,
        in_specs=(P(("grp", "cp"), None), P(("grp", "cp"), None), P(("grp", "cp"), None), P("grp")),
        out_specs=P(("grp", "cp"), None),
        check_vma=False,
    )
```

time: 138 us -> 59.9 us (0.43)
  the two profiles are of different devices: /device:TPU:6 before, /device:TPU:1 now
where the time goes in v1:
time: 59.9 us; the launch traced here: 59.8 us
  Pallas kernels  56.6 us (94%)
  local copies, waits for them, and re-layouts  3.16 us (5%)
    pallas_call x1, Pallas kernels, on_device(): pl.pallas_call(kernel, out_shape=jax.ShapeDtypeStruct(queries.shape, BF16...  56.6 us
    unnamed x1, local copies, waits for them, and re-layouts  3.16 us

profile of v1, /device:TPU:1, one launch (start us, length us, event | category | flops | bytes accessed | tf_op | source)
XLA Modules:
  0.0 59.8 jit_solution(381453516745029758)
XLA Ops:
  0.0 56.6 %shard_map.46 = bf16[512,2048]{1,0:T(8,128)(2,1)} custom-call(bf16[512,2048]{1,0:T(8,128)(2,1)} %q_hbm.1, bf16[512,1024]{1,0:T(8,128)(2,1)} %k_hbm.1, bf16[512,1024]{1,0:T(8,128)(2,1)} %v_hbm.1, s32[1,256]{1,0:T(1,128)} %bitcast.1), custom_call_target="tpu_custom_call" | custom-call | tf_op jit(solution)/shard_map/pallas_call | solution.py:272
  56.6 3.2 %copy.6 = bf16[512,2048]{1,0:T(8,128)(2,1)} copy(bf16[512,2048]{1,0:T(8,128)(2,1)} %shard_map.46) | data formatting | bytes 4194304

commit v2 on v1

v2 whole, which is shorter than its diff:
```python
import functools
import math

import jax
import jax.numpy as jnp
from jax import lax
from jax.experimental import pallas as pl
from jax.experimental.pallas import tpu as pltpu
from jax.sharding import PartitionSpec as P

DH = 128
T = 512
B = 128
LAG = 3
BIG = 32768.0
NEG = -1e30
SCALE = 144.0 ** (-0.5) * math.log2(math.e)
MESH = pl.DeviceIdType.MESH
F32, BF16, I32 = jnp.float32, jnp.bfloat16, jnp.int32


def stacked(pair):
    return jnp.concatenate([pair[:, :DH], pair[:, DH:]], axis=0)


def kernel(
    q_hbm, k_hbm, v_hbm, len_ref, o_hbm,
    kv, qv, qr, raw, msg, outv, stat_s, stat_r, augk, augq, augr, flags,
    loc_sem, q_send, q_recv, own_send, own_recv, msg_send, msg_recv,
    st_send, st_recv, fwd_send, fwd_recv, out_sem,
):
    hk = kv.shape[0]
    n = lax.axis_size("cp")
    me = lax.axis_index("cp")
    core = lax.rem(me, 2)
    chip = lax.div(me, 2)
    partner = me + 1 - 2 * core
    next_head = lax.rem(me + 2 - core, n)
    last_head = lax.rem(me + n - 2, n)
    last_tail = lax.rem(me + n - 1, n)
    own0 = pl.multiple_of(T + T * core, T)
    barrier = pltpu.get_barrier_semaphore()
    half = T // 2

    def lanes(h, width):
        return pl.ds(pl.multiple_of(h * width, DH), width)

    def local(h):
        mine = pl.ds(own0, T)
        return (
            pltpu.make_async_copy(k_hbm.at[:, lanes(h, DH)], kv.at[h, mine, pl.ds(0, DH)], loc_sem.at[0, h]),
            pltpu.make_async_copy(v_hbm.at[:, lanes(h, DH)], raw.at[h], loc_sem.at[1, h]),
            pltpu.make_async_copy(q_hbm.at[:, lanes(h, 2 * DH)], qv.at[h], loc_sem.at[2, h]),
        )

    def remote(src, dst, send, recv, to):
        return pltpu.make_async_remote_copy(src, dst, send, recv, device_id={"cp": to}, device_id_type=MESH)

    def send_q(h, part):
        src = q_hbm.at[pl.ds(part * half, half), lanes(h, 2 * DH)]
        return remote(src, qr.at[h], q_send.at[part, h], q_recv.at[h], (last_head, last_tail)[part])

    def send_own(h):
        mine = kv.at[h, pl.ds(own0, T)]
        return remote(mine, mine, own_send.at[h], own_recv.at[h], partner)

    def send_msg(h, part):
        dst = kv.at[h, pl.ds(part * half, half)]
        return remote(msg.at[h], dst, msg_send.at[h], msg_recv.at[part, h], next_head)

    def send_stat(h, part):
        return remote(stat_s.at[h], stat_r.at[part, h], st_send.at[h], st_recv.at[part, h], next_head)

    def forward(h):
        part = kv.at[h, pl.ds(0, T)]
        return remote(part, part, fwd_send.at[h], fwd_recv.at[h], partner)

    def put(h):
        return pltpu.make_async_copy(outv.at[h], o_hbm.at[:, lanes(h, 2 * DH)], out_sem.at[h])

    def every(body):
        def step(h, carry):
            body(h)
            return carry

        lax.fori_loop(0, hk, step, 0)

    @pl.when(core == 0)
    def _():
        for other in (last_head, last_tail, next_head, partner):
            pl.semaphore_signal(barrier, inc=1, device_id={"cp": other}, device_id_type=MESH)
        pl.semaphore_wait(barrier, 4)

        def start(h):
            send_q(h, 0).start()
            send_q(h, 1).start()

        every(start)

    @pl.when(core == 1)
    def _():
        for other in (next_head, partner):
            pl.semaphore_signal(barrier, inc=1, device_id={"cp": other}, device_id_type=MESH)
        pl.semaphore_wait(barrier, 2)

    def start_local(h):
        for copy in local(h):
            copy.start()

    every(start_local)

    lens = jnp.broadcast_to(len_ref[...], (8, len_ref.shape[1]))
    docs = lens.shape[1]
    upto = lax.broadcasted_iota(I32, (docs, docs), 0) <= lax.broadcasted_iota(I32, (docs, docs), 1)
    upto = jnp.where(upto, 1.0, 0.0).astype(BF16)
    high = lax.shift_right_logical(lens, 5).astype(F32).astype(BF16)
    low = (lens & 31).astype(F32).astype(BF16)
    ends = 32.0 * jnp.dot(high, upto, preferred_element_type=F32) + jnp.dot(low, upto, preferred_element_type=F32)
    ends = ends[0:1].astype(I32)
    ones = jnp.ones((docs, DH), BF16)

    def doc_of(pos):
        past = jnp.where(pos >= ends, 1.0, 0.0).astype(BF16)
        return jnp.dot(past, ones, preferred_element_type=F32)

    def doc_rows(base, rows):
        return doc_of(lax.broadcasted_iota(I32, (rows, docs), 0) + base)

    def doc_at(p):
        return doc_of(jnp.zeros((8, docs), I32) + p)

    def bits(doc):
        lane = lax.broadcasted_iota(I32, doc.shape, 1)
        return (lax.shift_right_logical(doc.astype(I32), lane & 7) & 1).astype(F32), lane

    def key_side(doc, hidden):
        b, lane = bits(doc)
        out = jnp.where(lane < 8, b - 1.0, jnp.where(lane < 16, -b, jnp.where(lane == 16, -hidden, 0.0)))
        return (out * BIG).astype(BF16)

    def query_side(doc):
        b, lane = bits(doc)
        return jnp.where(lane < 8, b, jnp.where(lane < 16, 1.0 - b, jnp.where(lane == 16, 1.0, 0.0))).astype(BF16)

    first = chip * (2 * T)
    inner = jnp.where(chip > 0, 1.0, 0.0)
    far_left = jnp.where(doc_at(first - T - 1) == doc_at(first), 1.0, 0.0) * inner
    far_right = jnp.where(doc_at(first + T - 1) == doc_at(first + 2 * T), 1.0, 0.0)
    flags[0] = far_left
    flags[1] = far_right
    hidden = jnp.maximum(far_left, 1.0 - inner)[0:1]
    for part in range(3):
        doc = doc_rows(first + (part - 1) * T, T)
        augk[part * T : (part + 1) * T] = key_side(doc, hidden if part == 0 else 0.0)
    augq[...] = query_side(doc_rows(me * T, T))
    augr[...] = query_side(doc_rows(first + 2 * T + core * half, half))

    ones_v = jnp.ones((16, 3 * T), BF16)
    column = lax.broadcasted_iota(I32, (B, 2 * B), 1)
    causal = lax.broadcasted_iota(I32, (B, 2 * B), 0) <= (column & (B - 1))

    def scores(h, pair, aug, lo, hi):
        q = jnp.concatenate([stacked(pair), jnp.concatenate([aug, aug], axis=0)], axis=1)
        k = jnp.concatenate([kv[h, lo:hi, 0:DH], augk[lo:hi]], axis=1)
        return lax.dot_general(k, q, (((1,), (1,)), ((), ())), preferred_element_type=F32)

    def mixed(h, s, top, lo, hi):
        p = jnp.exp2(s * SCALE - top).astype(BF16)
        v = jnp.concatenate([kv[h, i : i + B, DH : 2 * DH] for i in range(lo, hi, B)], axis=1)
        v = jnp.concatenate([v, ones_v[:, : hi - lo]], axis=0)
        o = jnp.dot(v, p, preferred_element_type=F32)
        return o[:DH], o[DH : DH + 1]

    def masked(s):
        return jnp.concatenate([s[:-B], jnp.where(causal, s[-B:], NEG)], axis=0)

    def store(h, r, o):
        rows = slice(r * B, (r + 1) * B)
        outv[h, rows, 0:DH] = jnp.transpose(o[:, :B]).astype(BF16)
        outv[h, rows, DH : 2 * DH] = jnp.transpose(o[:, B:]).astype(BF16)

    def border_block(h, i, part):
        rows = slice(i * B, (i + 1) * B)
        r = part * 2 + i
        lo, hi = T + r * B, 3 * T
        s = scores(h, qr[h, rows], augr[rows], lo, hi)
        top = jnp.max(s, axis=0, keepdims=True) * SCALE
        acc, total = mixed(h, s, top, lo, hi)
        own = kv[h, 2 * T + r * B : 2 * T + (r + 1) * B].astype(F32)
        msg[h, rows] = jnp.where(flags[1][0:1, 0:1] > 0.5, acc / total, own).astype(BF16)
        stat_s[h, i : i + 1] = top + jnp.log2(total)

    def border(h, part):
        send_q(h, part).wait_recv()
        send_own(h).wait_recv()
        for i in range(2):
            border_block(h, i, part)
        send_msg(h, part).start()
        send_stat(h, part).start()

    def head_block(h, r):
        rows = slice(r * B, (r + 1) * B)
        hi = T + (r + 1) * B
        s = masked(scores(h, qv[h, rows], augq[rows], 0, hi))
        level = jnp.where(flags[0][0:1, 0:1] > 0.5, stat_r[r // 2, h, r % 2 : r % 2 + 1], NEG)
        top = jnp.maximum(jnp.max(s, axis=0, keepdims=True) * SCALE, level)
        acc, total = mixed(h, s, top, 0, hi)
        weight = jnp.exp2(level - top)
        store(h, r, (acc + weight * kv[h, rows].astype(F32)) / (total + weight))

    def tail_block(h, r):
        rows = slice(r * B, (r + 1) * B)
        lo, hi = r * B, 2 * T + (r + 1) * B
        s = masked(scores(h, qv[h, rows], augq[rows], lo, hi))
        top = jnp.max(s, axis=0, keepdims=True) * SCALE
        acc, total = mixed(h, s, top, lo, hi)
        store(h, r, acc / total)

    def turn(h):
        for copy in local(h):
            copy.wait()
        for i in range(T // B):
            block = jnp.transpose(raw[h, i * B : (i + 1) * B].astype(F32)).astype(BF16)
            kv[h, pl.ds(pl.multiple_of(own0 + i * B, B), B), DH : 2 * DH] = block

    def share(h):
        @pl.when(h < hk)
        def _():
            turn(h)

        @pl.when(h > 0)
        def _():
            send_own(h - 1).start()

    def share_step(h, carry):
        share(h)
        return carry

    lax.fori_loop(0, hk + 1, share_step, 0)

    @pl.when(core == 0)
    def _():
        def step(it, carry):
            h = it - LAG

            @pl.when(it >= LAG)
            def _():
                for part in range(2):
                    send_msg(h, part).wait_recv()
                    send_stat(h, part).wait_recv()
                forward(h).start()

            @pl.when(it < hk)
            def _():
                border(it, 0)

            @pl.when(it >= LAG)
            def _():
                for r in range(T // B):
                    head_block(h, r)
                put(h).start()

            return carry

        lax.fori_loop(0, hk + LAG, step, 0)

        def finish(h):
            for part in range(2):
                send_q(h, part).wait_send()
            send_own(h).wait_send()
            send_msg(h, 0).wait_send()
            send_stat(h, 0).wait_send()
            forward(h).wait_send()
            put(h).wait()

        every(finish)

    @pl.when(core == 1)
    def _():
        def step(it, carry):
            h = it - LAG

            @pl.when(it < hk)
            def _():
                border(it, 1)

            @pl.when(it >= LAG)
            def _():
                forward(h).wait_recv()
                for r in range(T // B):
                    tail_block(h, r)
                put(h).start()

            return carry

        lax.fori_loop(0, hk + LAG, step, 0)

        def finish(h):
            send_own(h).wait_send()
            send_msg(h, 1).wait_send()
            send_stat(h, 1).wait_send()
            put(h).wait()

        every(finish)


def on_device(queries, keys, values, doc_lengths):
    hk = keys.shape[1] // DH
    docs = doc_lengths.shape[0]
    sem = pltpu.SemaphoreType.DMA
    any_spec = pl.BlockSpec(memory_space=pl.ANY)
    return pl.pallas_call(
        kernel,
        out_shape=jax.ShapeDtypeStruct(queries.shape, BF16),
        in_specs=[any_spec, any_spec, any_spec, pl.BlockSpec(memory_space=pltpu.VMEM)],
        out_specs=any_spec,
        scratch_shapes=[
            pltpu.VMEM((hk, 3 * T, 2 * DH), BF16),
            pltpu.VMEM((hk, T, 2 * DH), BF16),
            pltpu.VMEM((hk, T // 2, 2 * DH), BF16),
            pltpu.VMEM((hk, T, DH), BF16),
            pltpu.VMEM((hk, T // 2, 2 * DH), BF16),
            pltpu.VMEM((hk, T, 2 * DH), BF16),
            pltpu.VMEM((hk, 8, 2 * B), F32),
            pltpu.VMEM((2, hk, 8, 2 * B), F32),
            pltpu.VMEM((3 * T, DH), BF16),
            pltpu.VMEM((T, DH), BF16),
            pltpu.VMEM((T // 2, DH), BF16),
            pltpu.VMEM((2, 8, DH), F32),
            sem((3, hk)),
            sem((2, hk)),
            sem((hk,)),
            sem((hk,)),
            sem((hk,)),
            sem((hk,)),
            sem((2, hk)),
            sem((hk,)),
            sem((2, hk)),
            sem((hk,)),
            sem((hk,)),
            sem((hk,)),
        ],
        compiler_params=pltpu.CompilerParams(
            collective_id=0, has_side_effects=True, vmem_limit_bytes=60 * 1024 * 1024
        ),
    )(queries, keys, values, doc_lengths.reshape(1, docs))


def solution(mesh):
    return jax.shard_map(
        on_device,
        mesh=mesh,
        in_specs=(P(("grp", "cp"), None), P(("grp", "cp"), None), P(("grp", "cp"), None), P("grp")),
        out_specs=P(("grp", "cp"), None),
        check_vma=False,
    )
```

time: 59.9 us -> 64.1 us (1.070)
  Pallas kernels: 56.6 us -> 60.8 us
    pallas_call x1, Pallas kernels: 56.6 us -> 60.8 us  [on_device(): pl.pallas_call(kernel, out_shape=jax.ShapeDtypeStruct(queries.shape, BF16...]
where the time goes in v2:
time: 64.1 us; the launch traced here: 64 us
  Pallas kernels  60.8 us (95%)
  local copies, waits for them, and re-layouts  3.16 us (5%)
    pallas_call x1, Pallas kernels, on_device(): pl.pallas_call(kernel, out_shape=jax.ShapeDtypeStruct(queries.shape, BF16...  60.8 us
    unnamed x1, local copies, waits for them, and re-layouts  3.16 us

profile of v2, /device:TPU:1, one launch (start us, length us, event | category | flops | bytes accessed | tf_op | source)
XLA Modules:
  0.0 64.0 jit_solution(7749206495961169177)
XLA Ops:
  0.0 60.8 %shard_map.46 = bf16[512,2048]{1,0:T(8,128)(2,1)} custom-call(bf16[512,2048]{1,0:T(8,128)(2,1)} %q_hbm.1, bf16[512,1024]{1,0:T(8,128)(2,1)} %k_hbm.1, bf16[512,1024]{1,0:T(8,128)(2,1)} %v_hbm.1, s32[1,256]{1,0:T(1,128)} %bitcast.1), custom_call_target="tpu_custom_call" | custom-call | tf_op jit(solution)/shard_map/pallas_call | solution.py:312
  60.8 3.2 %copy.6 = bf16[512,2048]{1,0:T(8,128)(2,1)} copy(bf16[512,2048]{1,0:T(8,128)(2,1)} %shard_map.46) | data formatting | bytes 4194304

commit v3 on v2

--- a/solution.py
+++ b/solution.py
@@ -23,11 +23,15 @@
     return jnp.concatenate([pair[:, :DH], pair[:, DH:]], axis=0)
 
 
+def unstacked(x):
+    return jnp.concatenate([x[:B], x[B:]], axis=1)
+
+
 def kernel(
-    q_hbm, k_hbm, v_hbm, len_ref, o_hbm,
-    kv, qv, qr, raw, msg, outv, stat_s, stat_r, augk, augq, augr, flags,
+    q_hbm, k_hbm, v_hbm, len_ref, o_ref,
+    kv, qv, qr, msg, stat_s, stat_r, augk, augq, augr, flags,
     loc_sem, q_send, q_recv, own_send, own_recv, msg_send, msg_recv,
-    st_send, st_recv, fwd_send, fwd_recv, out_sem,
+    st_send, st_recv, fwd_send, fwd_recv,
 ):
     hk = kv.shape[0]
     n = lax.axis_size("cp")
@@ -49,7 +53,7 @@
         mine = pl.ds(own0, T)
         return (
             pltpu.make_async_copy(k_hbm.at[:, lanes(h, DH)], kv.at[h, mine, pl.ds(0, DH)], loc_sem.at[0, h]),
-            pltpu.make_async_copy(v_hbm.at[:, lanes(h, DH)], raw.at[h], loc_sem.at[1, h]),
+            pltpu.make_async_copy(v_hbm.at[:, lanes(h, DH)], kv.at[h, mine, pl.ds(DH, DH)], loc_sem.at[1, h]),
             pltpu.make_async_copy(q_hbm.at[:, lanes(h, 2 * DH)], qv.at[h], loc_sem.at[2, h]),
         )
 
@@ -74,9 +78,6 @@
     def forward(h):
         part = kv.at[h, pl.ds(0, T)]
         return remote(part, part, fwd_send.at[h], fwd_recv.at[h], partner)
-
-    def put(h):
-        return pltpu.make_async_copy(outv.at[h], o_hbm.at[:, lanes(h, 2 * DH)], out_sem.at[h])
 
     def every(body):
         def step(h, carry):
@@ -155,40 +156,36 @@
     augq[...] = query_side(doc_rows(me * T, T))
     augr[...] = query_side(doc_rows(first + 2 * T + core * half, half))
 
-    ones_v = jnp.ones((16, 3 * T), BF16)
-    column = lax.broadcasted_iota(I32, (B, 2 * B), 1)
-    causal = lax.broadcasted_iota(I32, (B, 2 * B), 0) <= (column & (B - 1))
+    ones_v = jnp.ones((3 * T, DH), BF16)
+    row = lax.broadcasted_iota(I32, (2 * B, B), 0)
+    causal = lax.broadcasted_iota(I32, (2 * B, B), 1) <= (row & (B - 1))
 
     def scores(h, pair, aug, lo, hi):
         q = jnp.concatenate([stacked(pair), jnp.concatenate([aug, aug], axis=0)], axis=1)
         k = jnp.concatenate([kv[h, lo:hi, 0:DH], augk[lo:hi]], axis=1)
-        return lax.dot_general(k, q, (((1,), (1,)), ((), ())), preferred_element_type=F32)
+        return lax.dot_general(q, k, (((1,), (1,)), ((), ())), preferred_element_type=F32)
 
     def mixed(h, s, top, lo, hi):
         p = jnp.exp2(s * SCALE - top).astype(BF16)
-        v = jnp.concatenate([kv[h, i : i + B, DH : 2 * DH] for i in range(lo, hi, B)], axis=1)
-        v = jnp.concatenate([v, ones_v[:, : hi - lo]], axis=0)
-        o = jnp.dot(v, p, preferred_element_type=F32)
-        return o[:DH], o[DH : DH + 1]
+        v = jnp.concatenate([kv[h, lo:hi, DH : 2 * DH], ones_v[: hi - lo]], axis=1)
+        o = jnp.dot(p, v, preferred_element_type=F32)
+        return o[:, :DH], o[:, DH:]
 
     def masked(s):
-        return jnp.concatenate([s[:-B], jnp.where(causal, s[-B:], NEG)], axis=0)
-
-    def store(h, r, o):
-        rows = slice(r * B, (r + 1) * B)
-        outv[h, rows, 0:DH] = jnp.transpose(o[:, :B]).astype(BF16)
-        outv[h, rows, DH : 2 * DH] = jnp.transpose(o[:, B:]).astype(BF16)
+        return jnp.concatenate([s[:, :-B], jnp.where(causal, s[:, -B:], NEG)], axis=1)
 
     def border_block(h, i, part):
         rows = slice(i * B, (i + 1) * B)
         r = part * 2 + i
         lo, hi = T + r * B, 3 * T
         s = scores(h, qr[h, rows], augr[rows], lo, hi)
-        top = jnp.max(s, axis=0, keepdims=True) * SCALE
+        top = jnp.max(s, axis=1, keepdims=True) * SCALE
         acc, total = mixed(h, s, top, lo, hi)
         own = kv[h, 2 * T + r * B : 2 * T + (r + 1) * B].astype(F32)
-        msg[h, rows] = jnp.where(flags[1][0:1, 0:1] > 0.5, acc / total, own).astype(BF16)
-        stat_s[h, i : i + 1] = top + jnp.log2(total)
+        msg[h, rows] = jnp.where(flags[1][0:1, 0:1] > 0.5, unstacked(acc / total), own).astype(BF16)
+        level = top + jnp.log2(total)
+        even = (lax.broadcasted_iota(I32, (B, DH), 1) & 1) == 0
+        stat_s[h, :, rows] = jnp.transpose(jnp.where(even, level[:B], level[B:]))[0:8]
 
     def border(h, part):
         send_q(h, part).wait_recv()
@@ -202,41 +199,31 @@
         rows = slice(r * B, (r + 1) * B)
         hi = T + (r + 1) * B
         s = masked(scores(h, qv[h, rows], augq[rows], 0, hi))
-        level = jnp.where(flags[0][0:1, 0:1] > 0.5, stat_r[r // 2, h, r % 2 : r % 2 + 1], NEG)
-        top = jnp.maximum(jnp.max(s, axis=0, keepdims=True) * SCALE, level)
+        part, at = r // 2, slice((r % 2) * B, (r % 2 + 1) * B)
+        level = jnp.concatenate(
+            [jnp.transpose(jnp.broadcast_to(stat_r[part, h, i : i + 1, at], (DH, B))) for i in range(2)], axis=0
+        )
+        level = jnp.where(flags[0][0:1] > 0.5, level, NEG)
+        top = jnp.maximum(jnp.max(s, axis=1, keepdims=True) * SCALE, level[:, 0:1])
         acc, total = mixed(h, s, top, 0, hi)
         weight = jnp.exp2(level - top)
-        store(h, r, (acc + weight * kv[h, rows].astype(F32)) / (total + weight))
+        other = stacked(kv[h, rows]).astype(F32)
+        o_ref[rows, lanes(h, 2 * DH)] = unstacked((acc + weight * other) / (total + weight)).astype(BF16)
 
     def tail_block(h, r):
         rows = slice(r * B, (r + 1) * B)
         lo, hi = r * B, 2 * T + (r + 1) * B
         s = masked(scores(h, qv[h, rows], augq[rows], lo, hi))
-        top = jnp.max(s, axis=0, keepdims=True) * SCALE
+        top = jnp.max(s, axis=1, keepdims=True) * SCALE
         acc, total = mixed(h, s, top, lo, hi)
-        store(h, r, acc / total)
-
-    def turn(h):
+        o_ref[rows, lanes(h, 2 * DH)] = unstacked(acc / total).astype(BF16)
+
+    def share(h):
         for copy in local(h):
             copy.wait()
-        for i in range(T // B):
-            block = jnp.transpose(raw[h, i * B : (i + 1) * B].astype(F32)).astype(BF16)
-            kv[h, pl.ds(pl.multiple_of(own0 + i * B, B), B), DH : 2 * DH] = block
-
-    def share(h):
-        @pl.when(h < hk)
-        def _():
-            turn(h)
-
-        @pl.when(h > 0)
-        def _():
-            send_own(h - 1).start()
-
-    def share_step(h, carry):
-        share(h)
-        return carry
-
-    lax.fori_loop(0, hk + 1, share_step, 0)
+        send_own(h).start()
+
+    every(share)
 
     @pl.when(core == 0)
     def _():
@@ -258,7 +245,6 @@
             def _():
                 for r in range(T // B):
                     head_block(h, r)
-                put(h).start()
 
             return carry
 
@@ -271,7 +257,6 @@
             send_msg(h, 0).wait_send()
             send_stat(h, 0).wait_send()
             forward(h).wait_send()
-            put(h).wait()
 
         every(finish)
 
@@ -289,7 +274,6 @@
                 forward(h).wait_recv()
                 for r in range(T // B):
                     tail_block(h, r)
-                put(h).start()
 
             return carry
 
@@ -299,7 +283,6 @@
             send_own(h).wait_send()
             send_msg(h, 1).wait_send()
             send_stat(h, 1).wait_send()
-            put(h).wait()
 
         every(finish)
 
@@ -308,19 +291,18 @@
     hk = keys.shape[1] // DH
     docs = doc_lengths.shape[0]
     sem = pltpu.SemaphoreType.DMA
-    any_spec = pl.BlockSpec(memory_space=pl.ANY)
+    hbm = pl.BlockSpec(memory_space=pltpu.HBM)
+    vmem = pl.BlockSpec(memory_space=pltpu.VMEM)
     return pl.pallas_call(
         kernel,
-        out_shape=jax.ShapeDtypeStruct(queries.shape, BF16),
-        in_specs=[any_spec, any_spec, any_spec, pl.BlockSpec(memory_space=pltpu.VMEM)],
-        out_specs=any_spec,
+        out_shape=pltpu.VMEM(queries.shape, BF16),
+        in_specs=[hbm, hbm, hbm, vmem],
+        out_specs=vmem,
         scratch_shapes=[
             pltpu.VMEM((hk, 3 * T, 2 * DH), BF16),
             pltpu.VMEM((hk, T, 2 * DH), BF16),
             pltpu.VMEM((hk, T // 2, 2 * DH), BF16),
-            pltpu.VMEM((hk, T, DH), BF16),
             pltpu.VMEM((hk, T // 2, 2 * DH), BF16),
-            pltpu.VMEM((hk, T, 2 * DH), BF16),
             pltpu.VMEM((hk, 8, 2 * B), F32),
             pltpu.VMEM((2, hk, 8, 2 * B), F32),
             pltpu.VMEM((3 * T, DH), BF16),
@@ -338,12 +320,11 @@
             sem((2, hk)),
             sem((hk,)),
             sem((hk,)),
-            sem((hk,)),
         ],
         compiler_params=pltpu.CompilerParams(
-            collective_id=0, has_side_effects=True, vmem_limit_bytes=60 * 1024 * 1024
+            collective_id=0, has_side_effects=True, vmem_limit_bytes=30 * 1024 * 1024
         ),
-    )(queries, keys, values, doc_lengths.reshape(1, docs))
+    )(*[pltpu.with_memory_space_constraint(x, pltpu.HBM) for x in (queries, keys, values, doc_lengths.reshape(1, docs))])
 
 
 def solution(mesh):

time: 64.1 us -> 51.7 us (0.81)
  Pallas kernels: 60.8 us -> 50.3 us
  local copies, waits for them, and re-layouts: 3.16 us -> 1.32 us
    pallas_call x1, Pallas kernels: 60.8 us -> 50.3 us  [on_device(): pl.pallas_call(kernel, out_shape=pltpu.VMEM(queries.shape, BF16), in_spec...]
    unnamed x1, local copies, waits for them, and re-layouts: 3.16 us -> 1.32 us
where the time goes in v3:
time: 51.7 us; the launch traced here: 51.6 us
  Pallas kernels  50.3 us (97%)
  local copies, waits for them, and re-layouts  1.32 us (3%)
    pallas_call x1, Pallas kernels, on_device(): pl.pallas_call(kernel, out_shape=pltpu.VMEM(queries.shape, BF16), in_spec...  50.3 us
    unnamed x1, local copies, waits for them, and re-layouts  1.32 us

profile of v3, /device:TPU:1, one launch (start us, length us, event | category | flops | bytes accessed | tf_op | source)
XLA Modules:
  0.0 51.6 jit_solution(5020518396758730966)
XLA Ops:
  0.0 50.3 %shard_map.46 = bf16[512,2048]{1,0:T(8,128)(2,1)S(1)} custom-call(bf16[512,2048]{1,0:T(8,128)(2,1)} %q_hbm.1, bf16[512,1024]{1,0:T(8,128)(2,1)} %k_hbm.1, bf16[512,1024]{1,0:T(8,128)(2,1)} %v_hbm.1, s32[1,256]{1,0:T(1,128)} %bitcast.1), custom_call_target="tpu_custom_call" | custom-call | tf_op jit(solution)/shard_map/pallas_call | solution.py:296
  50.3 1.3 %copy.6 = bf16[512,2048]{1,0:T(8,128)(2,1)} copy(bf16[512,2048]{1,0:T(8,128)(2,1)S(1)} %shard_map.46) | data formatting | bytes 4194304

commit v4 on v2

--- a/solution.py
+++ b/solution.py
@@ -11,7 +11,7 @@
 DH = 128
 T = 512
 B = 128
-LAG = 3
+LAG = 5
 BIG = 32768.0
 NEG = -1e30
 SCALE = 144.0 ** (-0.5) * math.log2(math.e)
@@ -24,10 +24,10 @@
 
 
 def kernel(
-    q_hbm, k_hbm, v_hbm, len_ref, o_hbm,
-    kv, qv, qr, raw, msg, outv, stat_s, stat_r, augk, augq, augr, flags,
+    q_hbm, k_hbm, v_hbm, len_ref, o_ref,
+    kv, qv, qr, raw, msg, stat_s, stat_r, augk, augq, augr, flags,
     loc_sem, q_send, q_recv, own_send, own_recv, msg_send, msg_recv,
-    st_send, st_recv, fwd_send, fwd_recv, out_sem,
+    st_send, st_recv, fwd_send, fwd_recv,
 ):
     hk = kv.shape[0]
     n = lax.axis_size("cp")
@@ -75,9 +75,6 @@
         part = kv.at[h, pl.ds(0, T)]
         return remote(part, part, fwd_send.at[h], fwd_recv.at[h], partner)
 
-    def put(h):
-        return pltpu.make_async_copy(outv.at[h], o_hbm.at[:, lanes(h, 2 * DH)], out_sem.at[h])
-
     def every(body):
         def step(h, carry):
             body(h)
@@ -85,29 +82,46 @@
 
         lax.fori_loop(0, hk, step, 0)
 
-    @pl.when(core == 0)
-    def _():
-        for other in (last_head, last_tail, next_head, partner):
-            pl.semaphore_signal(barrier, inc=1, device_id={"cp": other}, device_id_type=MESH)
-        pl.semaphore_wait(barrier, 4)
-
+    has_left = chip > 0
+    has_right = chip < lax.div(n, 2) - 1
+
+    def greet(other):
+        pl.semaphore_signal(barrier, inc=1, device_id={"cp": other}, device_id_type=MESH)
+
+    greet(partner)
+
+    @pl.when(has_right)
+    def _():
+        greet(next_head)
+
+    @pl.when(has_left & (core == 0))
+    def _():
+        greet(last_head)
+        greet(last_tail)
+
+    right, left = jnp.where(has_right, 1, 0), jnp.where(has_left, 1, 0)
+    pl.semaphore_wait(barrier, 1 + right + 2 * left * (1 - core))
+
+    @pl.when(has_left & (core == 0))
+    def _():
         def start(h):
             send_q(h, 0).start()
             send_q(h, 1).start()
 
         every(start)
 
-    @pl.when(core == 1)
-    def _():
-        for other in (next_head, partner):
-            pl.semaphore_signal(barrier, inc=1, device_id={"cp": other}, device_id_type=MESH)
-        pl.semaphore_wait(barrier, 2)
-
     def start_local(h):
         for copy in local(h):
             copy.start()
 
     every(start_local)
+
+    @pl.when(chip == 0)
+    def _():
+        def clear(h):
+            kv[h, 0:T] = jnp.zeros((T, 2 * DH), BF16)
+
+        every(clear)
 
     lens = jnp.broadcast_to(len_ref[...], (8, len_ref.shape[1]))
     docs = lens.shape[1]
@@ -176,14 +190,24 @@
 
     def store(h, r, o):
         rows = slice(r * B, (r + 1) * B)
-        outv[h, rows, 0:DH] = jnp.transpose(o[:, :B]).astype(BF16)
-        outv[h, rows, DH : 2 * DH] = jnp.transpose(o[:, B:]).astype(BF16)
+        o_ref[rows, lanes(2 * h, DH)] = jnp.transpose(o[:, :B]).astype(BF16)
+        o_ref[rows, lanes(2 * h + 1, DH)] = jnp.transpose(o[:, B:]).astype(BF16)
+
+    def staggered(blocks):
+        ahead = None
+        for block in [*blocks, None]:
+            if block is not None:
+                next(block)
+            if ahead is not None:
+                next(ahead, None)
+            ahead = block
 
     def border_block(h, i, part):
         rows = slice(i * B, (i + 1) * B)
         r = part * 2 + i
         lo, hi = T + r * B, 3 * T
         s = scores(h, qr[h, rows], augr[rows], lo, hi)
+        yield
         top = jnp.max(s, axis=0, keepdims=True) * SCALE
         acc, total = mixed(h, s, top, lo, hi)
         own = kv[h, 2 * T + r * B : 2 * T + (r + 1) * B].astype(F32)
@@ -192,9 +216,7 @@
 
     def border(h, part):
         send_q(h, part).wait_recv()
-        send_own(h).wait_recv()
-        for i in range(2):
-            border_block(h, i, part)
+        staggered(border_block(h, i, part) for i in range(2))
         send_msg(h, part).start()
         send_stat(h, part).start()
 
@@ -202,6 +224,7 @@
         rows = slice(r * B, (r + 1) * B)
         hi = T + (r + 1) * B
         s = masked(scores(h, qv[h, rows], augq[rows], 0, hi))
+        yield
         level = jnp.where(flags[0][0:1, 0:1] > 0.5, stat_r[r // 2, h, r % 2 : r % 2 + 1], NEG)
         top = jnp.maximum(jnp.max(s, axis=0, keepdims=True) * SCALE, level)
         acc, total = mixed(h, s, top, 0, hi)
@@ -212,6 +235,7 @@
         rows = slice(r * B, (r + 1) * B)
         lo, hi = r * B, 2 * T + (r + 1) * B
         s = masked(scores(h, qv[h, rows], augq[rows], lo, hi))
+        yield
         top = jnp.max(s, axis=0, keepdims=True) * SCALE
         acc, total = mixed(h, s, top, lo, hi)
         store(h, r, acc / total)
@@ -219,11 +243,11 @@
     def turn(h):
         for copy in local(h):
             copy.wait()
-        for i in range(T // B):
-            block = jnp.transpose(raw[h, i * B : (i + 1) * B].astype(F32)).astype(BF16)
-            kv[h, pl.ds(pl.multiple_of(own0 + i * B, B), B), DH : 2 * DH] = block
-
-    def share(h):
+        for i in range(0, T, DH):
+            block = jnp.transpose(raw[h, i : i + DH].astype(F32)).astype(BF16)
+            kv[h, pl.ds(pl.multiple_of(own0 + i, DH), DH), DH : 2 * DH] = block
+
+    def share(h, carry):
         @pl.when(h < hk)
         def _():
             turn(h)
@@ -232,18 +256,16 @@
         def _():
             send_own(h - 1).start()
 
-    def share_step(h, carry):
-        share(h)
         return carry
 
-    lax.fori_loop(0, hk + 1, share_step, 0)
+    lax.fori_loop(0, hk + 1, share, 0)
 
     @pl.when(core == 0)
     def _():
         def step(it, carry):
             h = it - LAG
 
-            @pl.when(it >= LAG)
+            @pl.when((it >= LAG) & has_left)
             def _():
                 for part in range(2):
                     send_msg(h, part).wait_recv()
@@ -252,26 +274,33 @@
 
             @pl.when(it < hk)
             def _():
-                border(it, 0)
+                send_own(it).wait_recv()
+
+                @pl.when(has_right)
+                def _():
+                    border(it, 0)
 
             @pl.when(it >= LAG)
             def _():
-                for r in range(T // B):
-                    head_block(h, r)
-                put(h).start()
+                staggered(head_block(h, r) for r in range(T // B))
 
             return carry
 
         lax.fori_loop(0, hk + LAG, step, 0)
 
         def finish(h):
-            for part in range(2):
-                send_q(h, part).wait_send()
             send_own(h).wait_send()
-            send_msg(h, 0).wait_send()
-            send_stat(h, 0).wait_send()
-            forward(h).wait_send()
-            put(h).wait()
+
+            @pl.when(has_left)
+            def _():
+                for part in range(2):
+                    send_q(h, part).wait_send()
+                forward(h).wait_send()
+
+            @pl.when(has_right)
+            def _():
+                send_msg(h, 0).wait_send()
+                send_stat(h, 0).wait_send()
 
         every(finish)
 
@@ -282,14 +311,19 @@
 
             @pl.when(it < hk)
             def _():
-                border(it, 1)
+                send_own(it).wait_recv()
+
+                @pl.when(has_right)
+                def _():
+                    border(it, 1)
 
             @pl.when(it >= LAG)
             def _():
-                forward(h).wait_recv()
-                for r in range(T // B):
-                    tail_block(h, r)
-                put(h).start()
+                @pl.when(has_left)
+                def _():
+                    forward(h).wait_recv()
+
+                staggered(tail_block(h, r) for r in range(T // B))
 
             return carry
 
@@ -297,9 +331,11 @@
 
         def finish(h):
             send_own(h).wait_send()
-            send_msg(h, 1).wait_send()
-            send_stat(h, 1).wait_send()
-            put(h).wait()
+
+            @pl.when(has_right)
+            def _():
+                send_msg(h, 1).wait_send()
+                send_stat(h, 1).wait_send()
 
         every(finish)
 
@@ -308,19 +344,19 @@
     hk = keys.shape[1] // DH
     docs = doc_lengths.shape[0]
     sem = pltpu.SemaphoreType.DMA
-    any_spec = pl.BlockSpec(memory_space=pl.ANY)
+    hbm = pl.BlockSpec(memory_space=pltpu.HBM)
+    vmem = pl.BlockSpec(memory_space=pltpu.VMEM)
     return pl.pallas_call(
         kernel,
-        out_shape=jax.ShapeDtypeStruct(queries.shape, BF16),
-        in_specs=[any_spec, any_spec, any_spec, pl.BlockSpec(memory_space=pltpu.VMEM)],
-        out_specs=any_spec,
+        out_shape=pltpu.VMEM(queries.shape, BF16),
+        in_specs=[hbm, hbm, hbm, vmem],
+        out_specs=vmem,
         scratch_shapes=[
             pltpu.VMEM((hk, 3 * T, 2 * DH), BF16),
             pltpu.VMEM((hk, T, 2 * DH), BF16),
             pltpu.VMEM((hk, T // 2, 2 * DH), BF16),
             pltpu.VMEM((hk, T, DH), BF16),
             pltpu.VMEM((hk, T // 2, 2 * DH), BF16),
-            pltpu.VMEM((hk, T, 2 * DH), BF16),
             pltpu.VMEM((hk, 8, 2 * B), F32),
             pltpu.VMEM((2, hk, 8, 2 * B), F32),
             pltpu.VMEM((3 * T, DH), BF16),
@@ -338,12 +374,11 @@
             sem((2, hk)),
             sem((hk,)),
             sem((hk,)),
-            sem((hk,)),
         ],
         compiler_params=pltpu.CompilerParams(
-            collective_id=0, has_side_effects=True, vmem_limit_bytes=60 * 1024 * 1024
+            collective_id=0, has_side_effects=True, vmem_limit_bytes=30 * 1024 * 1024
         ),
-    )(queries, keys, values, doc_lengths.reshape(1, docs))
+    )(*[pltpu.with_memory_space_constraint(x, pltpu.HBM) for x in (queries, keys, values, doc_lengths.reshape(1, docs))])
 
 
 def solution(mesh):

time: 64.1 us -> 48.8 us (0.76); the launches traced: 64 us -> 48 us
  Pallas kernels: 60.8 us -> 46.6 us
  local copies, waits for them, and re-layouts: 3.16 us -> 1.32 us
    pallas_call x1, Pallas kernels: 60.8 us -> 46.6 us  [on_device(): pl.pallas_call(kernel, out_shape=pltpu.VMEM(queries.shape, BF16), in_spec...]
    unnamed x1, local copies, waits for them, and re-layouts: 3.16 us -> 1.32 us
where the time goes in v4:
time: 48.8 us; the launch traced here: 48 us
  Pallas kernels  46.6 us (95%)
  local copies, waits for them, and re-layouts  1.32 us (3%)
    pallas_call x1, Pallas kernels, on_device(): pl.pallas_call(kernel, out_shape=pltpu.VMEM(queries.shape, BF16), in_spec...  46.6 us
    unnamed x1, local copies, waits for them, and re-layouts  1.32 us

profile of v4, /device:TPU:1, one launch (start us, length us, event | category | flops | bytes accessed | tf_op | source)
XLA Modules:
  0.0 48.0 jit_solution(14013528747646502901)
XLA Ops:
  0.0 46.6 %shard_map.46 = bf16[512,2048]{1,0:T(8,128)(2,1)S(1)} custom-call(bf16[512,2048]{1,0:T(8,128)(2,1)} %q_hbm.1, bf16[512,1024]{1,0:T(8,128)(2,1)} %k_hbm.1, bf16[512,1024]{1,0:T(8,128)(2,1)} %v_hbm.1, s32[1,256]{1,0:T(1,128)} %bitcast.1), custom_call_target="tpu_custom_call" | custom-call | tf_op jit(solution)/shard_map/pallas_call | solution.py:349
  46.6 1.3 %copy.6 = bf16[512,2048]{1,0:T(8,128)(2,1)} copy(bf16[512,2048]{1,0:T(8,128)(2,1)S(1)} %shard_map.46) | data formatting | bytes 4194304

commit v5 on v4

--- a/solution.py
+++ b/solution.py
@@ -11,7 +11,8 @@
 DH = 128
 T = 512
 B = 128
-LAG = 5
+C = 512
+LAG = 3
 BIG = 32768.0
 NEG = -1e30
 SCALE = 144.0 ** (-0.5) * math.log2(math.e)
@@ -25,7 +26,7 @@
 
 def kernel(
     q_hbm, k_hbm, v_hbm, len_ref, o_ref,
-    kv, qv, qr, raw, msg, stat_s, stat_r, augk, augq, augr, flags,
+    kv, qv, qr, raw, msg, held, tops, stat_s, stat_r, augk, augq, augr, flags,
     loc_sem, q_send, q_recv, own_send, own_recv, msg_send, msg_recv,
     st_send, st_recv, fwd_send, fwd_recv,
 ):
@@ -57,7 +58,7 @@
         return pltpu.make_async_remote_copy(src, dst, send, recv, device_id={"cp": to}, device_id_type=MESH)
 
     def send_q(h, part):
-        src = q_hbm.at[pl.ds(part * half, half), lanes(h, 2 * DH)]
+        src = qv.at[h, pl.ds(part * half, half)]
         return remote(src, qr.at[h], q_send.at[part, h], q_recv.at[h], (last_head, last_tail)[part])
 
     def send_own(h):
@@ -82,6 +83,15 @@
 
         lax.fori_loop(0, hk, step, 0)
 
+    def start_local(which):
+        def start(h):
+            local(h)[which].start()
+
+        return start
+
+    for which in (2, 1, 0):
+        every(start_local(which))
+
     has_left = chip > 0
     has_right = chip < lax.div(n, 2) - 1
 
@@ -102,19 +112,15 @@
     right, left = jnp.where(has_right, 1, 0), jnp.where(has_left, 1, 0)
     pl.semaphore_wait(barrier, 1 + right + 2 * left * (1 - core))
 
-    @pl.when(has_left & (core == 0))
-    def _():
-        def start(h):
+    def query(h):
+        local(h)[2].wait()
+
+        @pl.when(has_left & (core == 0))
+        def _():
             send_q(h, 0).start()
             send_q(h, 1).start()
 
-        every(start)
-
-    def start_local(h):
-        for copy in local(h):
-            copy.start()
-
-    every(start_local)
+    every(query)
 
     @pl.when(chip == 0)
     def _():
@@ -173,20 +179,34 @@
     column = lax.broadcasted_iota(I32, (B, 2 * B), 1)
     causal = lax.broadcasted_iota(I32, (B, 2 * B), 0) <= (column & (B - 1))
 
-    def scores(h, pair, aug, lo, hi):
+    def chunks(lo, hi):
+        return [(i, min(i + C, hi)) for i in range(lo, hi, C)]
+
+    def scores(h, pair, aug, lo, hi, diagonal):
         q = jnp.concatenate([stacked(pair), jnp.concatenate([aug, aug], axis=0)], axis=1)
-        k = jnp.concatenate([kv[h, lo:hi, 0:DH], augk[lo:hi]], axis=1)
-        return lax.dot_general(k, q, (((1,), (1,)), ((), ())), preferred_element_type=F32)
-
-    def mixed(h, s, top, lo, hi):
-        p = jnp.exp2(s * SCALE - top).astype(BF16)
-        v = jnp.concatenate([kv[h, i : i + B, DH : 2 * DH] for i in range(lo, hi, B)], axis=1)
-        v = jnp.concatenate([v, ones_v[:, : hi - lo]], axis=0)
-        o = jnp.dot(v, p, preferred_element_type=F32)
-        return o[:DH], o[DH : DH + 1]
-
-    def masked(s):
-        return jnp.concatenate([s[:-B], jnp.where(causal, s[-B:], NEG)], axis=0)
+        found, top = [], None
+        for i, j in chunks(lo, hi):
+            k = jnp.concatenate([kv[h, i:j, 0:DH], augk[i:j]], axis=1)
+            s = lax.dot_general(k, q, (((1,), (1,)), ((), ())), preferred_element_type=F32)
+            if diagonal and j == hi:
+                last = jnp.where(causal, s[-B:], NEG)
+                s = jnp.concatenate([s[:-B], last], axis=0) if j - i > B else last
+            high = jnp.max(s, axis=0, keepdims=True)
+            top = high if top is None else jnp.maximum(top, high)
+            found.append(s)
+            yield
+        return found, top * SCALE
+
+    def mixed(h, found, top, lo, hi):
+        o = None
+        for s, (i, j) in zip(found, chunks(lo, hi)):
+            p = jnp.exp2(s * SCALE - top).astype(BF16)
+            v = jnp.concatenate([kv[h, k : k + B, DH : 2 * DH] for k in range(i, j, B)], axis=1)
+            v = jnp.concatenate([v, ones_v[:, : j - i]], axis=0)
+            part = jnp.dot(v, p, preferred_element_type=F32)
+            o = part if o is None else o + part
+            yield
+        return o
 
     def store(h, r, o):
         rows = slice(r * B, (r + 1) * B)
@@ -194,22 +214,25 @@
         o_ref[rows, lanes(2 * h + 1, DH)] = jnp.transpose(o[:, B:]).astype(BF16)
 
     def staggered(blocks):
-        ahead = None
+        behind = None
         for block in [*blocks, None]:
             if block is not None:
-                next(block)
-            if ahead is not None:
-                next(ahead, None)
-            ahead = block
+                for _ in iter(lambda: next(block), "scored"):
+                    if behind is not None:
+                        next(behind, None)
+            if behind is not None:
+                for _ in behind:
+                    pass
+            behind = block
 
     def border_block(h, i, part):
         rows = slice(i * B, (i + 1) * B)
         r = part * 2 + i
         lo, hi = T + r * B, 3 * T
-        s = scores(h, qr[h, rows], augr[rows], lo, hi)
-        yield
-        top = jnp.max(s, axis=0, keepdims=True) * SCALE
-        acc, total = mixed(h, s, top, lo, hi)
+        s, top = yield from scores(h, qr[h, rows], augr[rows], lo, hi, False)
+        yield "scored"
+        o = yield from mixed(h, s, top, lo, hi)
+        acc, total = o[:DH], o[DH : DH + 1]
         own = kv[h, 2 * T + r * B : 2 * T + (r + 1) * B].astype(F32)
         msg[h, rows] = jnp.where(flags[1][0:1, 0:1] > 0.5, acc / total, own).astype(BF16)
         stat_s[h, i : i + 1] = top + jnp.log2(total)
@@ -220,28 +243,34 @@
         send_msg(h, part).start()
         send_stat(h, part).start()
 
-    def head_block(h, r):
+    def near_block(h, r, core):
         rows = slice(r * B, (r + 1) * B)
-        hi = T + (r + 1) * B
-        s = masked(scores(h, qv[h, rows], augq[rows], 0, hi))
-        yield
-        level = jnp.where(flags[0][0:1, 0:1] > 0.5, stat_r[r // 2, h, r % 2 : r % 2 + 1], NEG)
-        top = jnp.maximum(jnp.max(s, axis=0, keepdims=True) * SCALE, level)
-        acc, total = mixed(h, s, top, 0, hi)
-        weight = jnp.exp2(level - top)
-        store(h, r, (acc + weight * kv[h, rows].astype(F32)) / (total + weight))
-
-    def tail_block(h, r):
+        lo, hi = T, T + core * T + (r + 1) * B
+        s, top = yield from scores(h, qv[h, rows], augq[rows], lo, hi, True)
+        yield "scored"
+        held[h, r] = yield from mixed(h, s, top, lo, hi)
+        tops[h, r : r + 1] = top
+
+    def far_block(h, r, core):
         rows = slice(r * B, (r + 1) * B)
-        lo, hi = r * B, 2 * T + (r + 1) * B
-        s = masked(scores(h, qv[h, rows], augq[rows], lo, hi))
-        yield
-        top = jnp.max(s, axis=0, keepdims=True) * SCALE
-        acc, total = mixed(h, s, top, lo, hi)
+        lo, hi = core * r * B, T
+        s, top = yield from scores(h, qv[h, rows], augq[rows], lo, hi, False)
+        yield "scored"
+        before = tops[h, r : r + 1]
+        top = jnp.maximum(top, before)
+        if core == 0:
+            level = jnp.where(flags[0][0:1, 0:1] > 0.5, stat_r[r // 2, h, r % 2 : r % 2 + 1], NEG)
+            top = jnp.maximum(top, level)
+        o = yield from mixed(h, s, top, lo, hi)
+        o = o + held[h, r] * jnp.exp2(before - top)
+        acc, total = o[:DH], o[DH : DH + 1]
+        if core == 0:
+            weight = jnp.exp2(level - top)
+            acc, total = acc + weight * kv[h, rows].astype(F32), total + weight
         store(h, r, acc / total)
 
     def turn(h):
-        for copy in local(h):
+        for copy in local(h)[:2]:
             copy.wait()
         for i in range(0, T, DH):
             block = jnp.transpose(raw[h, i : i + DH].astype(F32)).astype(BF16)
@@ -280,9 +309,11 @@
                 def _():
                     border(it, 0)
 
+                staggered(near_block(it, r, 0) for r in range(T // B))
+
             @pl.when(it >= LAG)
             def _():
-                staggered(head_block(h, r) for r in range(T // B))
+                staggered(far_block(h, r, 0) for r in range(T // B))
 
             return carry
 
@@ -317,13 +348,15 @@
                 def _():
                     border(it, 1)
 
+                staggered(near_block(it, r, 1) for r in range(T // B))
+
             @pl.when(it >= LAG)
             def _():
                 @pl.when(has_left)
                 def _():
                     forward(h).wait_recv()
 
-                staggered(tail_block(h, r) for r in range(T // B))
+                staggered(far_block(h, r, 1) for r in range(T // B))
 
             return carry
 
@@ -357,6 +390,8 @@
             pltpu.VMEM((hk, T // 2, 2 * DH), BF16),
             pltpu.VMEM((hk, T, DH), BF16),
             pltpu.VMEM((hk, T // 2, 2 * DH), BF16),
+            pltpu.VMEM((hk, T // B, DH + 16, 2 * B), F32),
+            pltpu.VMEM((hk, 8, 2 * B), F32),
             pltpu.VMEM((hk, 8, 2 * B), F32),
             pltpu.VMEM((2, hk, 8, 2 * B), F32),
             pltpu.VMEM((3 * T, DH), BF16),
@@ -376,7 +411,7 @@
             sem((hk,)),
         ],
         compiler_params=pltpu.CompilerParams(
-            collective_id=0, has_side_effects=True, vmem_limit_bytes=30 * 1024 * 1024
+            collective_id=0, has_side_effects=True, vmem_limit_bytes=36 * 1024 * 1024
         ),
     )(*[pltpu.with_memory_space_constraint(x, pltpu.HBM) for x in (queries, keys, values, doc_lengths.reshape(1, docs))])
 

time: 48.8 us -> 46.3 us (0.949)
  the two profiles are of different devices: /device:TPU:1 before, /device:TPU:15 now
where the time goes in v5:
time: 46.3 us; the launch traced here: 46.2 us
  Pallas kernels  44.8 us (97%)
  local copies, waits for them, and re-layouts  1.32 us (3%)
    pallas_call x1, Pallas kernels, on_device(): pl.pallas_call(kernel, out_shape=pltpu.VMEM(queries.shape, BF16), in_spec...  44.8 us
    unnamed x1, local copies, waits for them, and re-layouts  1.32 us

profile of v5, /device:TPU:15, one launch (start us, length us, event | category | flops | bytes accessed | tf_op | source)
XLA Modules:
  0.0 46.2 jit_solution(17047441801308615588)
XLA Ops:
  0.0 44.8 %shard_map.46 = bf16[512,2048]{1,0:T(8,128)(2,1)S(1)} custom-call(bf16[512,2048]{1,0:T(8,128)(2,1)} %q_hbm.1, bf16[512,1024]{1,0:T(8,128)(2,1)} %k_hbm.1, bf16[512,1024]{1,0:T(8,128)(2,1)} %v_hbm.1, s32[1,256]{1,0:T(1,128)} %bitcast.1), custom_call_target="tpu_custom_call" | custom-call | tf_op jit(solution)/shard_map/pallas_call | solution.py:382
  44.8 1.3 %copy.6 = bf16[512,2048]{1,0:T(8,128)(2,1)} copy(bf16[512,2048]{1,0:T(8,128)(2,1)S(1)} %shard_map.46) | data formatting | bytes 4194304

commit v6 on v5

--- a/solution.py
+++ b/solution.py
@@ -13,6 +13,8 @@
 B = 128
 C = 512
 LAG = 3
+FIRST_LAG, LAST_LAG = 5, 6
+LINE = 8
 BIG = 32768.0
 NEG = -1e30
 SCALE = 144.0 ** (-0.5) * math.log2(math.e)
@@ -26,9 +28,9 @@
 
 def kernel(
     q_hbm, k_hbm, v_hbm, len_ref, o_ref,
-    kv, qv, qr, raw, msg, held, tops, stat_s, stat_r, augk, augq, augr, flags,
+    kv, qv, qr, raw, msg, held, tops, stat_s, stat_r, early, augk, augq, augr, flags,
     loc_sem, q_send, q_recv, own_send, own_recv, msg_send, msg_recv,
-    st_send, st_recv, fwd_send, fwd_recv,
+    st_send, st_recv, fwd_send, fwd_recv, whole_send, whole_recv,
 ):
     hk = kv.shape[0]
     n = lax.axis_size("cp")
@@ -72,6 +74,11 @@
     def send_stat(h, part):
         return remote(stat_s.at[h], stat_r.at[part, h], st_send.at[h], st_recv.at[part, h], next_head)
 
+    def send_whole(part):
+        src = kv.at[hk - 1, pl.ds(T + part * T, T)]
+        dst = (early, kv.at[hk - 1, pl.ds(0, T)])[part]
+        return remote(src, dst, whole_send, (whole_recv, msg_recv.at[0, hk - 1])[part], next_head)
+
     def forward(h):
         part = kv.at[h, pl.ds(0, T)]
         return remote(part, part, fwd_send.at[h], fwd_recv.at[h], partner)
@@ -92,6 +99,8 @@
     for which in (2, 1, 0):
         every(start_local(which))
 
+    place = lax.rem(chip, LINE)
+    lag = jnp.where(place == 0, FIRST_LAG, jnp.where(place == LINE - 1, LAST_LAG, LAG))
     has_left = chip > 0
     has_right = chip < lax.div(n, 2) - 1
 
@@ -117,8 +126,10 @@
 
         @pl.when(has_left & (core == 0))
         def _():
-            send_q(h, 0).start()
-            send_q(h, 1).start()
+            @pl.when(h < hk - 1)
+            def _():
+                send_q(h, 0).start()
+                send_q(h, 1).start()
 
     every(query)
 
@@ -128,6 +139,37 @@
             kv[h, 0:T] = jnp.zeros((T, 2 * DH), BF16)
 
         every(clear)
+        early[...] = jnp.zeros((T, 2 * DH), BF16)
+
+    def turn(h):
+        for copy in local(h)[:2]:
+            copy.wait()
+        for i in range(0, T, DH):
+            block = jnp.transpose(raw[h, i : i + DH].astype(F32)).astype(BF16)
+            kv[h, pl.ds(pl.multiple_of(own0 + i, DH), DH), DH : 2 * DH] = block
+
+    def share(i, carry):
+        @pl.when(i < hk)
+        def _():
+            turn(lax.rem(i + hk - 1, hk))
+
+        @pl.when(i > 0)
+        def _():
+            send_own(lax.rem(i + hk - 2, hk)).start()
+
+        @pl.when((i == 1) & has_right)
+        def _():
+            @pl.when(core == 0)
+            def _():
+                send_whole(0).start()
+
+            @pl.when(core == 1)
+            def _():
+                send_whole(1).start()
+
+        return carry
+
+    lax.fori_loop(0, hk + 1, share, 0)
 
     lens = jnp.broadcast_to(len_ref[...], (8, len_ref.shape[1]))
     docs = lens.shape[1]
@@ -172,6 +214,9 @@
     for part in range(3):
         doc = doc_rows(first + (part - 1) * T, T)
         augk[part * T : (part + 1) * T] = key_side(doc, hidden if part == 0 else 0.0)
+        if part == 0:
+            augk[4 * T : 5 * T] = key_side(doc, 1.0 - inner)
+    augk[3 * T : 4 * T] = key_side(doc_rows(first - 2 * T, T), 1.0 - inner)
     augq[...] = query_side(doc_rows(me * T, T))
     augr[...] = query_side(doc_rows(first + 2 * T + core * half, half))
 
@@ -180,17 +225,25 @@
     causal = lax.broadcasted_iota(I32, (B, 2 * B), 0) <= (column & (B - 1))
 
     def chunks(lo, hi):
+        if lo < 0 < hi:
+            return chunks(lo, 0) + chunks(0, hi)
         return [(i, min(i + C, hi)) for i in range(lo, hi, C)]
 
-    def scores(h, pair, aug, lo, hi, diagonal):
+    def rows_of(h, i, j):
+        return early[i + T : j + T] if i < 0 else kv[h, i:j]
+
+    def aug_of(i, j, last):
+        return augk[i + 4 * T : j + 4 * T] if last and j <= T else augk[i:j]
+
+    def scores(h, pair, aug, lo, hi, diagonal, last=False):
         q = jnp.concatenate([stacked(pair), jnp.concatenate([aug, aug], axis=0)], axis=1)
         found, top = [], None
         for i, j in chunks(lo, hi):
-            k = jnp.concatenate([kv[h, i:j, 0:DH], augk[i:j]], axis=1)
+            k = jnp.concatenate([rows_of(h, i, j)[:, 0:DH], aug_of(i, j, last)], axis=1)
             s = lax.dot_general(k, q, (((1,), (1,)), ((), ())), preferred_element_type=F32)
             if diagonal and j == hi:
-                last = jnp.where(causal, s[-B:], NEG)
-                s = jnp.concatenate([s[:-B], last], axis=0) if j - i > B else last
+                end = jnp.where(causal, s[-B:], NEG)
+                s = jnp.concatenate([s[:-B], end], axis=0) if j - i > B else end
             high = jnp.max(s, axis=0, keepdims=True)
             top = high if top is None else jnp.maximum(top, high)
             found.append(s)
@@ -201,7 +254,7 @@
         o = None
         for s, (i, j) in zip(found, chunks(lo, hi)):
             p = jnp.exp2(s * SCALE - top).astype(BF16)
-            v = jnp.concatenate([kv[h, k : k + B, DH : 2 * DH] for k in range(i, j, B)], axis=1)
+            v = jnp.concatenate([rows_of(h, k, k + B)[:, DH : 2 * DH] for k in range(i, j, B)], axis=1)
             v = jnp.concatenate([v, ones_v[:, : j - i]], axis=0)
             part = jnp.dot(v, p, preferred_element_type=F32)
             o = part if o is None else o + part
@@ -251,106 +304,108 @@
         held[h, r] = yield from mixed(h, s, top, lo, hi)
         tops[h, r : r + 1] = top
 
-    def far_block(h, r, core):
+    def far_block(h, r, core, last=False):
         rows = slice(r * B, (r + 1) * B)
         lo, hi = core * r * B, T
-        s, top = yield from scores(h, qv[h, rows], augq[rows], lo, hi, False)
+        if last and core == 0:
+            lo = r * B - T
+        s, top = yield from scores(h, qv[h, rows], augq[rows], lo, hi, False, last)
         yield "scored"
         before = tops[h, r : r + 1]
         top = jnp.maximum(top, before)
-        if core == 0:
+        if core == 0 and not last:
             level = jnp.where(flags[0][0:1, 0:1] > 0.5, stat_r[r // 2, h, r % 2 : r % 2 + 1], NEG)
             top = jnp.maximum(top, level)
         o = yield from mixed(h, s, top, lo, hi)
         o = o + held[h, r] * jnp.exp2(before - top)
         acc, total = o[:DH], o[DH : DH + 1]
-        if core == 0:
+        if core == 0 and not last:
             weight = jnp.exp2(level - top)
             acc, total = acc + weight * kv[h, rows].astype(F32), total + weight
         store(h, r, acc / total)
 
-    def turn(h):
-        for copy in local(h)[:2]:
-            copy.wait()
-        for i in range(0, T, DH):
-            block = jnp.transpose(raw[h, i : i + DH].astype(F32)).astype(BF16)
-            kv[h, pl.ds(pl.multiple_of(own0 + i, DH), DH), DH : 2 * DH] = block
-
-    def share(h, carry):
-        @pl.when(h < hk)
-        def _():
-            turn(h)
-
-        @pl.when(h > 0)
-        def _():
-            send_own(h - 1).start()
-
-        return carry
-
-    lax.fori_loop(0, hk + 1, share, 0)
-
     @pl.when(core == 0)
     def _():
         def step(it, carry):
-            h = it - LAG
-
-            @pl.when((it >= LAG) & has_left)
+            h = it - lag
+
+            @pl.when((it >= lag) & (h < hk - 1) & has_left)
             def _():
                 for part in range(2):
                     send_msg(h, part).wait_recv()
                     send_stat(h, part).wait_recv()
                 forward(h).start()
 
+            @pl.when((it == min(4, hk - 1)) & has_left)
+            def _():
+                send_whole(1).wait_recv()
+                forward(hk - 1).start()
+
             @pl.when(it < hk)
             def _():
                 send_own(it).wait_recv()
 
-                @pl.when(has_right)
+                @pl.when(has_right & (it < hk - 1))
                 def _():
                     border(it, 0)
 
                 staggered(near_block(it, r, 0) for r in range(T // B))
 
-            @pl.when(it >= LAG)
+            @pl.when((it >= lag) & (h < hk - 1))
             def _():
                 staggered(far_block(h, r, 0) for r in range(T // B))
 
+            @pl.when(it == hk - 1)
+            def _():
+                @pl.when(has_left)
+                def _():
+                    send_whole(0).wait_recv()
+
+                staggered(far_block(hk - 1, r, 0, True) for r in range(T // B))
+
             return carry
 
-        lax.fori_loop(0, hk + LAG, step, 0)
+        lax.fori_loop(0, hk + LAST_LAG - 1, step, 0)
 
         def finish(h):
             send_own(h).wait_send()
 
             @pl.when(has_left)
             def _():
+                forward(h).wait_send()
+
+            @pl.when(has_left & (h < hk - 1))
+            def _():
                 for part in range(2):
                     send_q(h, part).wait_send()
-                forward(h).wait_send()
-
-            @pl.when(has_right)
+
+            @pl.when(has_right & (h < hk - 1))
             def _():
                 send_msg(h, 0).wait_send()
                 send_stat(h, 0).wait_send()
+
+            @pl.when(has_right & (h == hk - 1))
+            def _():
+                send_whole(0).wait_send()
 
         every(finish)
 
     @pl.when(core == 1)
     def _():
         def step(it, carry):
-            h = it - LAG
+            h = it - lag
 
             @pl.when(it < hk)
             def _():
                 send_own(it).wait_recv()
 
-                @pl.when(has_right)
+                @pl.when(has_right & (it < hk - 1))
                 def _():
                     border(it, 1)
 
                 staggered(near_block(it, r, 1) for r in range(T // B))
 
-            @pl.when(it >= LAG)
+            @pl.when((it >= lag) & (h < hk - 1))
             def _():
                 @pl.when(has_left)
                 def _():
@@ -358,17 +413,29 @@
 
                 staggered(far_block(h, r, 1) for r in range(T // B))
 
+            @pl.when(it == hk - 1)
+            def _():
+                @pl.when(has_left)
+                def _():
+                    forward(hk - 1).wait_recv()
+
+                staggered(far_block(hk - 1, r, 1, True) for r in range(T // B))
+
             return carry
 
-        lax.fori_loop(0, hk + LAG, step, 0)
+        lax.fori_loop(0, hk + LAST_LAG - 1, step, 0)
 
         def finish(h):
             send_own(h).wait_send()
 
-            @pl.when(has_right)
+            @pl.when(has_right & (h < hk - 1))
             def _():
                 send_msg(h, 1).wait_send()
                 send_stat(h, 1).wait_send()
+
+            @pl.when(has_right & (h == hk - 1))
+            def _():
+                send_whole(1).wait_send()
 
         every(finish)
 
@@ -394,7 +461,8 @@
             pltpu.VMEM((hk, 8, 2 * B), F32),
             pltpu.VMEM((hk, 8, 2 * B), F32),
             pltpu.VMEM((2, hk, 8, 2 * B), F32),
-            pltpu.VMEM((3 * T, DH), BF16),
+            pltpu.VMEM((T, 2 * DH), BF16),
+            pltpu.VMEM((5 * T, DH), BF16),
             pltpu.VMEM((T, DH), BF16),
             pltpu.VMEM((T // 2, DH), BF16),
             pltpu.VMEM((2, 8, DH), F32),
@@ -409,6 +477,8 @@
             sem((2, hk)),
             sem((hk,)),
             sem((hk,)),
+            sem,
+            sem,
         ],
         compiler_params=pltpu.CompilerParams(
             collective_id=0, has_side_effects=True, vmem_limit_bytes=36 * 1024 * 1024

time: 46.3 us -> 42.7 us (0.922)
  the two profiles are of different devices: /device:TPU:15 before, /device:TPU:23 now
where the time goes in v6:
time: 42.7 us; the launch traced here: 42.6 us
  Pallas kernels  41.3 us (97%)
  local copies, waits for them, and re-layouts  1.32 us (3%)
    pallas_call x1, Pallas kernels, on_device(): pl.pallas_call(kernel, out_shape=pltpu.VMEM(queries.shape, BF16), in_spec...  41.3 us
    unnamed x1, local copies, waits for them, and re-layouts  1.32 us

profile of v6, /device:TPU:23, one launch (start us, length us, event | category | flops | bytes accessed | tf_op | source)
XLA Modules:
  0.0 42.6 jit_solution(2207793952703608977)
XLA Ops:
  0.0 41.3 %shard_map.46 = bf16[512,2048]{1,0:T(8,128)(2,1)S(1)} custom-call(bf16[512,2048]{1,0:T(8,128)(2,1)} %q_hbm.1, bf16[512,1024]{1,0:T(8,128)(2,1)} %k_hbm.1, bf16[512,1024]{1,0:T(8,128)(2,1)} %v_hbm.1, s32[1,256]{1,0:T(1,128)} %bitcast.1), custom_call_target="tpu_custom_call" | custom-call | tf_op jit(solution)/shard_map/pallas_call | solution.py:449
  41.3 1.3 %copy.6 = bf16[512,2048]{1,0:T(8,128)(2,1)} copy(bf16[512,2048]{1,0:T(8,128)(2,1)S(1)} %shard_map.46) | data formatting | bytes 4194304

commit v7 on v6

--- a/solution.py
+++ b/solution.py
@@ -11,9 +11,9 @@
 DH = 128
 T = 512
 B = 128
-C = 512
+BORDER, NEAR, FAR, WHOLE = 512, (256, 512), 256, 512
 LAG = 3
-FIRST_LAG, LAST_LAG = 5, 6
+FIRST_LAG, LAST_LAG = 4, 5
 LINE = 8
 BIG = 32768.0
 NEG = -1e30
@@ -27,10 +27,10 @@
 
 
 def kernel(
-    q_hbm, k_hbm, v_hbm, len_ref, o_ref,
-    kv, qv, qr, raw, msg, held, tops, stat_s, stat_r, early, augk, augq, augr, flags,
+    q_hbm, k_hbm, v_hbm, len_hbm, o_ref,
+    kv, qv, qr, raw, msg, held, tops, stat_s, stat_r, early, augk, augq, augr, flags, len_ref,
     loc_sem, q_send, q_recv, own_send, own_recv, msg_send, msg_recv,
-    st_send, st_recv, fwd_send, fwd_recv, whole_send, whole_recv,
+    st_send, st_recv, fwd_send, fwd_recv, whole_send, whole_recv, len_sem,
 ):
     hk = kv.shape[0]
     n = lax.axis_size("cp")
@@ -96,6 +96,8 @@
 
         return start
 
+    lengths = pltpu.make_async_copy(len_hbm, len_ref, len_sem)
+    lengths.start()
     for which in (2, 1, 0):
         every(start_local(which))
 
@@ -171,6 +173,7 @@
 
     lax.fori_loop(0, hk + 1, share, 0)
 
+    lengths.wait()
     lens = jnp.broadcast_to(len_ref[...], (8, len_ref.shape[1]))
     docs = lens.shape[1]
     upto = lax.broadcasted_iota(I32, (docs, docs), 0) <= lax.broadcasted_iota(I32, (docs, docs), 1)
@@ -224,10 +227,10 @@
     column = lax.broadcasted_iota(I32, (B, 2 * B), 1)
     causal = lax.broadcasted_iota(I32, (B, 2 * B), 0) <= (column & (B - 1))
 
-    def chunks(lo, hi):
+    def chunks(lo, hi, size):
         if lo < 0 < hi:
-            return chunks(lo, 0) + chunks(0, hi)
-        return [(i, min(i + C, hi)) for i in range(lo, hi, C)]
+            return chunks(lo, 0, size) + chunks(0, hi, size)
+        return [(i, min(i + size, hi)) for i in range(lo, hi, size)]
 
     def rows_of(h, i, j):
         return early[i + T : j + T] if i < 0 else kv[h, i:j]
@@ -235,10 +238,10 @@
     def aug_of(i, j, last):
         return augk[i + 4 * T : j + 4 * T] if last and j <= T else augk[i:j]
 
-    def scores(h, pair, aug, lo, hi, diagonal, last=False):
+    def scores(h, pair, aug, lo, hi, size, diagonal, last=False):
         q = jnp.concatenate([stacked(pair), jnp.concatenate([aug, aug], axis=0)], axis=1)
         found, top = [], None
-        for i, j in chunks(lo, hi):
+        for i, j in chunks(lo, hi, size):
             k = jnp.concatenate([rows_of(h, i, j)[:, 0:DH], aug_of(i, j, last)], axis=1)
             s = lax.dot_general(k, q, (((1,), (1,)), ((), ())), preferred_element_type=F32)
             if diagonal and j == hi:
@@ -250,9 +253,9 @@
             yield
         return found, top * SCALE
 
-    def mixed(h, found, top, lo, hi):
+    def mixed(h, found, top, lo, hi, size):
         o = None
-        for s, (i, j) in zip(found, chunks(lo, hi)):
+        for s, (i, j) in zip(found, chunks(lo, hi, size)):
             p = jnp.exp2(s * SCALE - top).astype(BF16)
             v = jnp.concatenate([rows_of(h, k, k + B)[:, DH : 2 * DH] for k in range(i, j, B)], axis=1)
             v = jnp.concatenate([v, ones_v[:, : j - i]], axis=0)
@@ -267,24 +270,25 @@
         o_ref[rows, lanes(2 * h + 1, DH)] = jnp.transpose(o[:, B:]).astype(BF16)
 
     def staggered(blocks):
-        behind = None
-        for block in [*blocks, None]:
+        behind = []
+        for block in [*blocks, None, None]:
             if block is not None:
                 for _ in iter(lambda: next(block), "scored"):
-                    if behind is not None:
-                        next(behind, None)
-            if behind is not None:
-                for _ in behind:
+                    if len(behind) > 1:
+                        next(behind[0], None)
+            if len(behind) > 1 or (block is None and behind):
+                for _ in behind.pop(0):
                     pass
-            behind = block
+            if block is not None:
+                behind.append(block)
 
     def border_block(h, i, part):
         rows = slice(i * B, (i + 1) * B)
         r = part * 2 + i
         lo, hi = T + r * B, 3 * T
-        s, top = yield from scores(h, qr[h, rows], augr[rows], lo, hi, False)
+        s, top = yield from scores(h, qr[h, rows], augr[rows], lo, hi, BORDER, False)
         yield "scored"
-        o = yield from mixed(h, s, top, lo, hi)
+        o = yield from mixed(h, s, top, lo, hi, BORDER)
         acc, total = o[:DH], o[DH : DH + 1]
         own = kv[h, 2 * T + r * B : 2 * T + (r + 1) * B].astype(F32)
         msg[h, rows] = jnp.where(flags[1][0:1, 0:1] > 0.5, acc / total, own).astype(BF16)
@@ -299,24 +303,24 @@
     def near_block(h, r, core):
         rows = slice(r * B, (r + 1) * B)
         lo, hi = T, T + core * T + (r + 1) * B
-        s, top = yield from scores(h, qv[h, rows], augq[rows], lo, hi, True)
+        s, top = yield from scores(h, qv[h, rows], augq[rows], lo, hi, NEAR[core], True)
         yield "scored"
-        held[h, r] = yield from mixed(h, s, top, lo, hi)
+        held[h, r] = yield from mixed(h, s, top, lo, hi, NEAR[core])
         tops[h, r : r + 1] = top
 
     def far_block(h, r, core, last=False):
         rows = slice(r * B, (r + 1) * B)
-        lo, hi = core * r * B, T
+        lo, hi, size = core * r * B, T, WHOLE if last else FAR
         if last and core == 0:
             lo = r * B - T
-        s, top = yield from scores(h, qv[h, rows], augq[rows], lo, hi, False, last)
+        s, top = yield from scores(h, qv[h, rows], augq[rows], lo, hi, size, False, last)
         yield "scored"
         before = tops[h, r : r + 1]
         top = jnp.maximum(top, before)
         if core == 0 and not last:
             level = jnp.where(flags[0][0:1, 0:1] > 0.5, stat_r[r // 2, h, r % 2 : r % 2 + 1], NEG)
             top = jnp.maximum(top, level)
-        o = yield from mixed(h, s, top, lo, hi)
+        o = yield from mixed(h, s, top, lo, hi, size)
         o = o + held[h, r] * jnp.exp2(before - top)
         acc, total = o[:DH], o[DH : DH + 1]
         if core == 0 and not last:
@@ -349,7 +353,7 @@
                 def _():
                     border(it, 0)
 
-                staggered(near_block(it, r, 0) for r in range(T // B))
+                staggered(near_block(it, r, 0) for r in reversed(range(T // B)))
 
             @pl.when((it >= lag) & (h < hk - 1))
             def _():
@@ -365,7 +369,7 @@
 
             return carry
 
-        lax.fori_loop(0, hk + LAST_LAG - 1, step, 0)
+        lax.fori_loop(0, hk + max(FIRST_LAG, LAST_LAG) - 1, step, 0)
 
         def finish(h):
             send_own(h).wait_send()
@@ -403,7 +407,7 @@
                 def _():
                     border(it, 1)
 
-                staggered(near_block(it, r, 1) for r in range(T // B))
+                staggered(near_block(it, r, 1) for r in reversed(range(T // B)))
 
             @pl.when((it >= lag) & (h < hk - 1))
             def _():
@@ -423,7 +427,7 @@
 
             return carry
 
-        lax.fori_loop(0, hk + LAST_LAG - 1, step, 0)
+        lax.fori_loop(0, hk + max(FIRST_LAG, LAST_LAG) - 1, step, 0)
 
         def finish(h):
             send_own(h).wait_send()
@@ -449,7 +453,7 @@
     return pl.pallas_call(
         kernel,
         out_shape=pltpu.VMEM(queries.shape, BF16),
-        in_specs=[hbm, hbm, hbm, vmem],
+        in_specs=[hbm, hbm, hbm, hbm],
         out_specs=vmem,
         scratch_shapes=[
             pltpu.VMEM((hk, 3 * T, 2 * DH), BF16),
@@ -466,6 +470,7 @@
             pltpu.VMEM((T, DH), BF16),
             pltpu.VMEM((T // 2, DH), BF16),
             pltpu.VMEM((2, 8, DH), F32),
+            pltpu.VMEM((1, docs), I32),
             sem((3, hk)),
             sem((2, hk)),
             sem((hk,)),
@@ -477,6 +482,7 @@
             sem((2, hk)),
             sem((hk,)),
             sem((hk,)),
+            sem,
             sem,
             sem,
         ],

time: 42.7 us -> 42.1 us (0.986)
  Pallas kernels: 41.3 us -> 40.7 us
    pallas_call x1, Pallas kernels: 41.3 us -> 40.7 us  [on_device(): pl.pallas_call(kernel, out_shape=pltpu.VMEM(queries.shape, BF16), in_spec...]
where the time goes in v7:
time: 42.1 us; the launch traced here: 42 us
  Pallas kernels  40.7 us (97%)
  local copies, waits for them, and re-layouts  1.32 us (3%)
    pallas_call x1, Pallas kernels, on_device(): pl.pallas_call(kernel, out_shape=pltpu.VMEM(queries.shape, BF16), in_spec...  40.7 us
    unnamed x1, local copies, waits for them, and re-layouts  1.32 us

profile of v7, /device:TPU:23, one launch (start us, length us, event | category | flops | bytes accessed | tf_op | source)
XLA Modules:
  0.0 42.0 jit_solution(13205688129611366097)
XLA Ops:
  0.0 40.7 %shard_map.46 = bf16[512,2048]{1,0:T(8,128)(2,1)S(1)} custom-call(bf16[512,2048]{1,0:T(8,128)(2,1)} %q_hbm.1, bf16[512,1024]{1,0:T(8,128)(2,1)} %k_hbm.1, bf16[512,1024]{1,0:T(8,128)(2,1)} %v_hbm.1, s32[1,256]{1,0:T(1,128)} %bitcast.1), custom_call_target="tpu_custom_call" | custom-call | tf_op jit(solution)/shard_map/pallas_call | solution.py:453
  40.7 1.3 %copy.6 = bf16[512,2048]{1,0:T(8,128)(2,1)} copy(bf16[512,2048]{1,0:T(8,128)(2,1)S(1)} %shard_map.46) | data formatting | bytes 4194304

commit v8 on v7

--- a/solution.py
+++ b/solution.py
@@ -79,9 +79,9 @@
         dst = (early, kv.at[hk - 1, pl.ds(0, T)])[part]
         return remote(src, dst, whole_send, (whole_recv, msg_recv.at[0, hk - 1])[part], next_head)
 
-    def forward(h):
-        part = kv.at[h, pl.ds(0, T)]
-        return remote(part, part, fwd_send.at[h], fwd_recv.at[h], partner)
+    def forward(h, part):
+        rows = kv.at[h, pl.ds(part * half, half)]
+        return remote(rows, rows, fwd_send.at[part, h], fwd_recv.at[part, h], partner)
 
     def every(body):
         def step(h, carry):
@@ -292,7 +292,7 @@
         acc, total = o[:DH], o[DH : DH + 1]
         own = kv[h, 2 * T + r * B : 2 * T + (r + 1) * B].astype(F32)
         msg[h, rows] = jnp.where(flags[1][0:1, 0:1] > 0.5, acc / total, own).astype(BF16)
-        stat_s[h, i : i + 1] = top + jnp.log2(total)
+        stat_s[h, :, i * 2 * B : (i + 1) * 2 * B] = top + jnp.log2(total)
 
     def border(h, part):
         send_q(h, part).wait_recv()
@@ -318,7 +318,8 @@
         before = tops[h, r : r + 1]
         top = jnp.maximum(top, before)
         if core == 0 and not last:
-            level = jnp.where(flags[0][0:1, 0:1] > 0.5, stat_r[r // 2, h, r % 2 : r % 2 + 1], NEG)
+            i = r % 2 * 2 * B
+            level = jnp.where(flags[0][0:1, 0:1] > 0.5, stat_r[r // 2, h, :, i : i + 2 * B], NEG)
             top = jnp.maximum(top, level)
         o = yield from mixed(h, s, top, lo, hi, size)
         o = o + held[h, r] * jnp.exp2(before - top)
@@ -337,13 +338,15 @@
             def _():
                 for part in range(2):
                     send_msg(h, part).wait_recv()
+                    forward(h, part).start()
+                for part in range(2):
                     send_stat(h, part).wait_recv()
-                forward(h).start()
 
             @pl.when((it == min(4, hk - 1)) & has_left)
             def _():
                 send_whole(1).wait_recv()
-                forward(hk - 1).start()
+                for part in range(2):
+                    forward(hk - 1, part).start()
 
             @pl.when(it < hk)
             def _():
@@ -376,7 +379,8 @@
 
             @pl.when(has_left)
             def _():
-                forward(h).wait_send()
+                for part in range(2):
+                    forward(h, part).wait_send()
 
             @pl.when(has_left & (h < hk - 1))
             def _():
@@ -413,7 +417,8 @@
             def _():
                 @pl.when(has_left)
                 def _():
-                    forward(h).wait_recv()
+                    for part in range(2):
+                        forward(h, part).wait_recv()
 
                 staggered(far_block(h, r, 1) for r in range(T // B))
 
@@ -421,7 +426,8 @@
             def _():
                 @pl.when(has_left)
                 def _():
-                    forward(hk - 1).wait_recv()
+                    for part in range(2):
+                        forward(hk - 1, part).wait_recv()
 
                 staggered(far_block(hk - 1, r, 1, True) for r in range(T // B))
 
@@ -463,8 +469,8 @@
             pltpu.VMEM((hk, T // 2, 2 * DH), BF16),
             pltpu.VMEM((hk, T // B, DH + 16, 2 * B), F32),
             pltpu.VMEM((hk, 8, 2 * B), F32),
-            pltpu.VMEM((hk, 8, 2 * B), F32),
-            pltpu.VMEM((2, hk, 8, 2 * B), F32),
+            pltpu.VMEM((hk, 1, 4 * B), F32),
+            pltpu.VMEM((2, hk, 1, 4 * B), F32),
             pltpu.VMEM((T, 2 * DH), BF16),
             pltpu.VMEM((5 * T, DH), BF16),
             pltpu.VMEM((T, DH), BF16),
@@ -480,8 +486,8 @@
             sem((2, hk)),
             sem((hk,)),
             sem((2, hk)),
-            sem((hk,)),
-            sem((hk,)),
+            sem((2, hk)),
+            sem((2, hk)),
             sem,
             sem,
             sem,

time: 42.1 us -> 41.1 us (0.976)
  Pallas kernels: 40.7 us -> 39.7 us
    pallas_call x1, Pallas kernels: 40.7 us -> 39.7 us  [on_device(): pl.pallas_call(kernel, out_shape=pltpu.VMEM(queries.shape, BF16), in_spec...]
where the time goes in v8:
time: 41.1 us; the launch traced here: 41 us
  Pallas kernels  39.7 us (97%)
  local copies, waits for them, and re-layouts  1.32 us (3%)
    pallas_call x1, Pallas kernels, on_device(): pl.pallas_call(kernel, out_shape=pltpu.VMEM(queries.shape, BF16), in_spec...  39.7 us
    unnamed x1, local copies, waits for them, and re-layouts  1.32 us

profile of v8, /device:TPU:23, one launch (start us, length us, event | category | flops | bytes accessed | tf_op | source)
XLA Modules:
  0.0 41.0 jit_solution(3524041363342139455)
XLA Ops:
  0.0 39.7 %shard_map.46 = bf16[512,2048]{1,0:T(8,128)(2,1)S(1)} custom-call(bf16[512,2048]{1,0:T(8,128)(2,1)} %q_hbm.1, bf16[512,1024]{1,0:T(8,128)(2,1)} %k_hbm.1, bf16[512,1024]{1,0:T(8,128)(2,1)} %v_hbm.1, s32[1,256]{1,0:T(1,128)} %bitcast.1), custom_call_target="tpu_custom_call" | custom-call | tf_op jit(solution)/shard_map/pallas_call | solution.py:459
  39.7 1.3 %copy.6 = bf16[512,2048]{1,0:T(8,128)(2,1)} copy(bf16[512,2048]{1,0:T(8,128)(2,1)S(1)} %shard_map.46) | data formatting | bytes 4194304
